TPU v7x, 128 devices: a whole 4x4x4 slice. The times are simulated.
128 devices in a mesh: batch: 32 (over z, y_hi, x), head: 4 (over y_lo, core).
Axes of the slice: x: 4, y: 4 (y_hi: 2, y_lo: 2; y = y_hi * 2 + y_lo), z: 4, core: 2. Of those that a mesh axis runs over, the one named last changes fastest.
Arguments:
- features: bfloat16 [4096, 24, 512], P(('batch', 'head')), may hold values from -6 to 6
- state_h: bfloat16 [4096, 1024], P(('batch', 'head')), may hold values from -0.8984375 to 0.8984375
- state_c: bfloat16 [4096, 1024], P(('batch', 'head')), may hold values from -4 to 4
- valid: int32 [4096], P(('batch', 'head')), may hold values 0 or 1
- ends: int32 [4096, 24], P(('batch', 'head')), may hold values 0 or 1
- policy: int32 [4096, 1], P(('batch', 'head')), may hold values from 0 to 31; in each aligned block of 32 rows (0 to 31, 32 to 63, ...) at most 2 rows name the same one
- actions: int32 [4096, 16], P(('batch', 'head')), may hold values from 0 to 17
- w_input: bfloat16 [512, 4, 1024], P('batch', None, 'head'), may hold values from -0.25 to 0.25
- w_recur: bfloat16 [1024, 4, 1024], P('batch', None, 'head'), may hold values from -0.1875 to 0.1875
- lstm_bias: float32 [4, 1024], replicated, may hold values from -3 to 5
- w_hidden: bfloat16 [32, 1024, 1024], P('head'), may hold values from -0.1875 to 0.1875
- w_value: bfloat16 [32, 512], P('head'), may hold values from -0.25 to 0.25
- w_advantage: bfloat16 [32, 512, 18], P('head'), may hold values from -0.25 to 0.25
Outputs:
- q_values: float32 [4096, 16, 18], P(('batch', 'head'))
- q_taken: float32 [4096, 16], P(('batch', 'head'))
Inputs may be any that keep to these rules, and one draw needn't show every extreme that they name: In the rows of one device no policy appears more than 2 times, and some policy appears exactly 2 times.
All inputs are finite; a program needn't handle non-finite values. No bound on the sum of `valid` or of `ends` on one device may be relied on, other than what follows from the above.
Results may differ from a plain program's by a relative error of at most 0.007.
Values may be sent and summed in bfloat16 or wider, within the bound.
A program may use at most 128 MiB of HBM per device.

v0:
```python
import jax
import jax.numpy as jnp
from jax import lax
from jax.sharding import PartitionSpec as P

ACTIONS = 18
POLICIES = 32
CAPP = 2


def in_one_piece(arrays, axis, dim, along):
    widths = [a.shape[along] for a in arrays]
    both = jnp.concatenate(arrays, axis=along)
    filled = lax.all_gather(both, axis, axis=dim, tiled=True)
    return tuple(jnp.split(filled, [sum(widths[:k]) for k in range(1, len(widths))], axis=along))


def slot_table(owners, per_source, capacity, policies):
    count = owners.shape[0]
    sources = count // per_source
    place = jnp.arange(count, dtype=jnp.int32)
    anchor = place // per_source
    before = (
        (owners[:, None] == owners[None, :])
        & (anchor[:, None] == anchor[None, :])
        & (place[None, :] < place[:, None])
    )
    rank = jnp.sum(before.astype(jnp.int32), axis=1)
    target = owners * (sources * capacity) + anchor * capacity + rank
    total = policies * sources * capacity
    return (jnp.arange(total, dtype=jnp.int32)[:, None] == target[None, :]).astype(jnp.bfloat16)


def lstm_cell(pre_t, full_h, cell_state, keep_t, w_flat, bias, width):
    full_h = full_h * keep_t[:, None].astype(jnp.bfloat16)
    cell_state = cell_state * keep_t[:, None]
    gates = (
        pre_t
        + jnp.dot(full_h, w_flat, preferred_element_type=jnp.float32).reshape(-1, 4, width)
        + bias
    )
    cell_state = jax.nn.sigmoid(gates[:, 1]) * cell_state + jax.nn.sigmoid(gates[:, 0]) * jnp.tanh(
        gates[:, 2]
    )
    new_h = (jax.nn.sigmoid(gates[:, 3]) * jnp.tanh(cell_state)).astype(jnp.bfloat16)
    return (new_h, cell_state)


def shards(
    features,
    state_h,
    state_c,
    valid,
    ends,
    policy,
    actions,
    w_input,
    w_recur,
    lstm_bias,
    w_hidden,
    w_value,
    w_advantage,
):
    seq_dev, steps, width_e = features.shape
    width_h = state_h.shape[1]
    learn = actions.shape[1]
    burn = steps - learn
    keep_start = valid.astype(jnp.bfloat16)[:, None]
    start_h = state_h * keep_start
    start_c = state_c * keep_start
    w_in_rows, w_rec_rows = in_one_piece((w_input, w_recur), "head", 2, 0)
    feat_flat = features.transpose(1, 0, 2).reshape(-1, width_e)
    w_in_full = lax.all_gather(w_in_rows, "batch", axis=0, tiled=True).reshape(width_e, 4 * width_h)
    pre = jnp.dot(feat_flat, w_in_full, preferred_element_type=jnp.float32).reshape(
        steps, seq_dev, 4, width_h
    )
    w_flat = lax.all_gather(w_rec_rows, "batch", axis=0, tiled=True).reshape(width_h, 4 * width_h)
    keeps = 1.0 - ends.astype(jnp.float32).T

    def advance(carry, inputs):
        full_h, cell_state = carry
        pre_t, keep_t = inputs
        new_h, cell_state = lstm_cell(pre_t, full_h, cell_state, keep_t, w_flat, lstm_bias, width_h)
        return ((new_h, cell_state), new_h)

    _, outputs = lax.scan(advance, (start_h, start_c.astype(jnp.float32)), (pre, keeps))
    learned = outputs[burn:]
    table = slot_table(policy[:, 0], seq_dev, CAPP, POLICIES)
    packed = jnp.einsum("ks,tsu->ktu", table, learned, preferred_element_type=jnp.float32).astype(
        jnp.bfloat16
    )
    packed = packed.reshape(POLICIES, CAPP, learn, width_h)
    routed = lax.all_to_all(packed, "head", split_axis=0, concat_axis=1, tiled=True)
    local_heads, slots = (routed.shape[0], routed.shape[1])
    rows = routed.reshape(local_heads, slots * learn, width_h)
    mid = jnp.einsum("prh,phk->prk", rows, w_hidden, preferred_element_type=jnp.float32)
    mid = jnp.maximum(mid, 0.0).astype(jnp.bfloat16)
    branch = w_value.shape[1]
    value = jnp.einsum(
        "prk,pk->pr", mid[:, :, :branch], w_value, preferred_element_type=jnp.float32
    )
    advantage = jnp.einsum(
        "prk,pka->pra", mid[:, :, branch:], w_advantage, preferred_element_type=jnp.float32
    )
    q_local = value[:, :, None] + advantage - jnp.mean(advantage, axis=-1, keepdims=True)
    q_local = q_local.reshape(local_heads, slots, learn, ACTIONS)
    returned = lax.all_to_all(
        q_local.astype(jnp.bfloat16), "head", split_axis=1, concat_axis=0, tiled=True
    ).astype(q_local.dtype)
    own_table = slot_table(policy[:, 0], seq_dev, CAPP, POLICIES).astype(jnp.float32)
    q_values = jnp.dot(
        own_table.T,
        returned.reshape(POLICIES * CAPP, learn * ACTIONS),
        precision=lax.Precision.HIGHEST,
    ).reshape(seq_dev, learn, ACTIONS)
    chosen = actions[:, :, None] == jnp.arange(ACTIONS, dtype=jnp.int32)[None, None, :]
    q_taken = jnp.sum(jnp.where(chosen, q_values, 0.0), axis=-1)
    return (q_values, q_taken)


def solution(mesh):
    return jax.shard_map(
        shards,
        mesh=mesh,
        in_specs=(
            P(("batch", "head"), None, None),
            P(("batch", "head"), None),
            P(("batch", "head"), None),
            P(("batch", "head")),
            P(("batch", "head"), None),
            P(("batch", "head"), None),
            P(("batch", "head"), None),
            P("batch", None, "head"),
            P("batch", None, "head"),
            P(),
            P("head", None, None),
            P("head", None),
            P("head", None, None),
        ),
        out_specs=(P(("batch", "head"), None, None), P(("batch", "head"), None)),
        check_vma=False,
    )
```

profile of v0, /device:TPU:1, one launch (start us, length us, event | category | flops | bytes accessed | tf_op | source)
XLA Modules:
  0.0 450.7 jit_solution(334485971511818191)
XLA Ops:
  8.3 7.9 %all_gather.9 = bf16[48,4,1024]{2,1,0:T(4,128)(2,1)S(1)} all-gather(bf16[48,4,256]{2,1,0:T(4,128)(2,1)S(1)} %pad_maximum_fusion), channel_id=1, replica_groups=mesh['batch'=32,'head'=4] {'head'}, dimensions={2}, use_global_device_ids=true | all-gather | bytes 491520 | tf_op jit(solution)/shard_map/all_gather | solution.py:14
  18.4 79.2 %all-gather.3.cloned.1.call-done = bf16[512,4,1024]{2,1,0:T(4,128)(2,1)} async-done(((bf16[16,4,1024]{2,1,0:T(4,128)(2,1)}), bf16[512,4,1024]{2,1,0:T(4,128)(2,1)}) %all-gather.3.cloned.1.call-update) | async-done | bytes 4194320 | tf_op jit(solution)/shard_map/all_gather | solution.py:73
  102.1 6.6 %convolution_bitcast_fusion = f32[768,4096]{0,1:T(8,128)} fusion(bf16[512,4096]{1,0:T(8,128)(2,1)S(1)} %bitcast.92, bf16[768,512]{1,0:T(8,128)(2,1)S(1)} %bitcast.96), kind=kOutput, calls=%fused_computation.30 | convolution fusion | flops 3221225472 | bytes 17563648 | tf_op jit(solution)/shard_map/dot_general | solution.py:74
  108.7 12.7 %copy.47 = f32[768,4096]{1,0:T(8,128)} copy(f32[768,4096]{0,1:T(8,128)} %convolution_bitcast_fusion) | data formatting | bytes 25165824 | tf_op jit(solution)/shard_map/dot_general | solution.py:74
  121.3 15.6 %reshape.110 = f32[24,32,4,1024]{3,2,1,0:T(4,128)} reshape(f32[768,4096]{1,0:T(8,128)} %copy.47) | data formatting | bytes 25165824 | tf_op jit(solution)/shard_map/reshape | solution.py:74
  137.0 65.1 %all-gather.5.cloned.1.call-done = bf16[1024,4,1024]{2,1,0:T(4,128)(2,1)} async-done(((bf16[32,4,1024]{2,1,0:T(4,128)(2,1)}), bf16[1024,4,1024]{2,1,0:T(4,128)(2,1)}) %all-gather.5.cloned.1.call-update) | async-done | bytes 8388624 | tf_op jit(solution)/shard_map/all_gather | solution.py:77
  202.1 12.1 %copy.62 = bf16[128,8,4,1024]{3,1,2,0:T(8,128)(2,1)} copy(bf16[128,8,4,1024]{3,2,1,0:T(4,128)(2,1)} %bitcast.89) | data formatting | bytes 16777216
  214.2 173.0 %while.14 = (s32[]{:T(128)}, bf16[32,1024]{1,0:T(8,128)(2,1)S(1)}, f32[32,1024]{1,0:T(8,128)S(1)}, bf16[24,32,1024]{2,1,0:T(8,128)(2,1)}, f32[24,32,4,1024]{3,2,...) while((s32[]{:T(128)}, bf16[32,1024]{1,0:T(8,128)(2,1)S(1)}, ...), condition=%wide.region_2.3_spmd, body=%wide.region_1.2_spmd.sunk | while | flops 269221920 | bytes 12534885 | solution.py:86
  214.2 5.0 %fusion.55 = f32[32,4096]{1,0:T(8,128)S(1)} fusion(bf16[1024,4096]{1,0:T(8,128)(2,1)} %get-tuple-element.171, bf16[32,1024]{1,0:T(8,128)(2,1)S(1)} %get-tuple-element.157, bf16[32]{0:T(256)(128)(2,1)S(1)} %get-tuple-element.142), kind=kOutput, calls=%fused_computation.24.clone.1 | convolution fusion | flops 268468224 | bytes 8978496 | tf_op jit(solution)/shard_map/while/body/eval_jaxpr/dot_general | solution.py:39
  221.4 5.0 %fusion.55 = f32[32,4096]{1,0:T(8,128)S(1)} fusion(bf16[1024,4096]{1,0:T(8,128)(2,1)} %get-tuple-element.171, bf16[32,1024]{1,0:T(8,128)(2,1)S(1)} %get-tuple-element.157, bf16[32]{0:T(256)(128)(2,1)S(1)} %get-tuple-element.142), kind=kOutput, calls=%fused_computation.24.clone.1 | convolution fusion | flops 268468224 | bytes 8978496 | tf_op jit(solution)/shard_map/while/body/eval_jaxpr/dot_general | solution.py:39
  228.6 5.0 %fusion.55 = f32[32,4096]{1,0:T(8,128)S(1)} fusion(bf16[1024,4096]{1,0:T(8,128)(2,1)} %get-tuple-element.171, bf16[32,1024]{1,0:T(8,128)(2,1)S(1)} %get-tuple-element.157, bf16[32]{0:T(256)(128)(2,1)S(1)} %get-tuple-element.142), kind=kOutput, calls=%fused_computation.24.clone.1 | convolution fusion | flops 268468224 | bytes 8978496 | tf_op jit(solution)/shard_map/while/body/eval_jaxpr/dot_general | solution.py:39
  243.0 5.0 %fusion.55 = f32[32,4096]{1,0:T(8,128)S(1)} fusion(bf16[1024,4096]{1,0:T(8,128)(2,1)} %get-tuple-element.171, bf16[32,1024]{1,0:T(8,128)(2,1)S(1)} %get-tuple-element.157, bf16[32]{0:T(256)(128)(2,1)S(1)} %get-tuple-element.142), kind=kOutput, calls=%fused_computation.24.clone.1 | convolution fusion | flops 268468224 | bytes 8978496 | tf_op jit(solution)/shard_map/while/body/eval_jaxpr/dot_general | solution.py:39
  250.2 5.0 %fusion.55 = f32[32,4096]{1,0:T(8,128)S(1)} fusion(bf16[1024,4096]{1,0:T(8,128)(2,1)} %get-tuple-element.171, bf16[32,1024]{1,0:T(8,128)(2,1)S(1)} %get-tuple-element.157, bf16[32]{0:T(256)(128)(2,1)S(1)} %get-tuple-element.142), kind=kOutput, calls=%fused_computation.24.clone.1 | convolution fusion | flops 268468224 | bytes 8978496 | tf_op jit(solution)/shard_map/while/body/eval_jaxpr/dot_general | solution.py:39
  264.6 5.0 %fusion.55 = f32[32,4096]{1,0:T(8,128)S(1)} fusion(bf16[1024,4096]{1,0:T(8,128)(2,1)} %get-tuple-element.171, bf16[32,1024]{1,0:T(8,128)(2,1)S(1)} %get-tuple-element.157, bf16[32]{0:T(256)(128)(2,1)S(1)} %get-tuple-element.142), kind=kOutput, calls=%fused_computation.24.clone.1 | convolution fusion | flops 268468224 | bytes 8978496 | tf_op jit(solution)/shard_map/while/body/eval_jaxpr/dot_general | solution.py:39
  271.9 5.0 %fusion.55 = f32[32,4096]{1,0:T(8,128)S(1)} fusion(bf16[1024,4096]{1,0:T(8,128)(2,1)} %get-tuple-element.171, bf16[32,1024]{1,0:T(8,128)(2,1)S(1)} %get-tuple-element.157, bf16[32]{0:T(256)(128)(2,1)S(1)} %get-tuple-element.142), kind=kOutput, calls=%fused_computation.24.clone.1 | convolution fusion | flops 268468224 | bytes 8978496 | tf_op jit(solution)/shard_map/while/body/eval_jaxpr/dot_general | solution.py:39
  279.1 5.0 %fusion.55 = f32[32,4096]{1,0:T(8,128)S(1)} fusion(bf16[1024,4096]{1,0:T(8,128)(2,1)} %get-tuple-element.171, bf16[32,1024]{1,0:T(8,128)(2,1)S(1)} %get-tuple-element.157, bf16[32]{0:T(256)(128)(2,1)S(1)} %get-tuple-element.142), kind=kOutput, calls=%fused_computation.24.clone.1 | convolution fusion | flops 268468224 | bytes 8978496 | tf_op jit(solution)/shard_map/while/body/eval_jaxpr/dot_general | solution.py:39
  286.3 5.0 %fusion.55 = f32[32,4096]{1,0:T(8,128)S(1)} fusion(bf16[1024,4096]{1,0:T(8,128)(2,1)} %get-tuple-element.171, bf16[32,1024]{1,0:T(8,128)(2,1)S(1)} %get-tuple-element.157, bf16[32]{0:T(256)(128)(2,1)S(1)} %get-tuple-element.142), kind=kOutput, calls=%fused_computation.24.clone.1 | convolution fusion | flops 268468224 | bytes 8978496 | tf_op jit(solution)/shard_map/while/body/eval_jaxpr/dot_general | solution.py:39
  293.5 5.0 %fusion.55 = f32[32,4096]{1,0:T(8,128)S(1)} fusion(bf16[1024,4096]{1,0:T(8,128)(2,1)} %get-tuple-element.171, bf16[32,1024]{1,0:T(8,128)(2,1)S(1)} %get-tuple-element.157, bf16[32]{0:T(256)(128)(2,1)S(1)} %get-tuple-element.142), kind=kOutput, calls=%fused_computation.24.clone.1 | convolution fusion | flops 268468224 | bytes 8978496 | tf_op jit(solution)/shard_map/while/body/eval_jaxpr/dot_general | solution.py:39
  300.7 5.0 %fusion.55 = f32[32,4096]{1,0:T(8,128)S(1)} fusion(bf16[1024,4096]{1,0:T(8,128)(2,1)} %get-tuple-element.171, bf16[32,1024]{1,0:T(8,128)(2,1)S(1)} %get-tuple-element.157, bf16[32]{0:T(256)(128)(2,1)S(1)} %get-tuple-element.142), kind=kOutput, calls=%fused_computation.24.clone.1 | convolution fusion | flops 268468224 | bytes 8978496 | tf_op jit(solution)/shard_map/while/body/eval_jaxpr/dot_general | solution.py:39
  307.9 5.0 %fusion.55 = f32[32,4096]{1,0:T(8,128)S(1)} fusion(bf16[1024,4096]{1,0:T(8,128)(2,1)} %get-tuple-element.171, bf16[32,1024]{1,0:T(8,128)(2,1)S(1)} %get-tuple-element.157, bf16[32]{0:T(256)(128)(2,1)S(1)} %get-tuple-element.142), kind=kOutput, calls=%fused_computation.24.clone.1 | convolution fusion | flops 268468224 | bytes 8978496 | tf_op jit(solution)/shard_map/while/body/eval_jaxpr/dot_general | solution.py:39
  315.1 5.0 %fusion.55 = f32[32,4096]{1,0:T(8,128)S(1)} fusion(bf16[1024,4096]{1,0:T(8,128)(2,1)} %get-tuple-element.171, bf16[32,1024]{1,0:T(8,128)(2,1)S(1)} %get-tuple-element.157, bf16[32]{0:T(256)(128)(2,1)S(1)} %get-tuple-element.142), kind=kOutput, calls=%fused_computation.24.clone.1 | convolution fusion | flops 268468224 | bytes 8978496 | tf_op jit(solution)/shard_map/while/body/eval_jaxpr/dot_general | solution.py:39
  322.3 5.0 %fusion.55 = f32[32,4096]{1,0:T(8,128)S(1)} fusion(bf16[1024,4096]{1,0:T(8,128)(2,1)} %get-tuple-element.171, bf16[32,1024]{1,0:T(8,128)(2,1)S(1)} %get-tuple-element.157, bf16[32]{0:T(256)(128)(2,1)S(1)} %get-tuple-element.142), kind=kOutput, calls=%fused_computation.24.clone.1 | convolution fusion | flops 268468224 | bytes 8978496 | tf_op jit(solution)/shard_map/while/body/eval_jaxpr/dot_general | solution.py:39
  329.5 5.0 %fusion.55 = f32[32,4096]{1,0:T(8,128)S(1)} fusion(bf16[1024,4096]{1,0:T(8,128)(2,1)} %get-tuple-element.171, bf16[32,1024]{1,0:T(8,128)(2,1)S(1)} %get-tuple-element.157, bf16[32]{0:T(256)(128)(2,1)S(1)} %get-tuple-element.142), kind=kOutput, calls=%fused_computation.24.clone.1 | convolution fusion | flops 268468224 | bytes 8978496 | tf_op jit(solution)/shard_map/while/body/eval_jaxpr/dot_general | solution.py:39
  336.7 5.0 %fusion.55 = f32[32,4096]{1,0:T(8,128)S(1)} fusion(bf16[1024,4096]{1,0:T(8,128)(2,1)} %get-tuple-element.171, bf16[32,1024]{1,0:T(8,128)(2,1)S(1)} %get-tuple-element.157, bf16[32]{0:T(256)(128)(2,1)S(1)} %get-tuple-element.142), kind=kOutput, calls=%fused_computation.24.clone.1 | convolution fusion | flops 268468224 | bytes 8978496 | tf_op jit(solution)/shard_map/while/body/eval_jaxpr/dot_general | solution.py:39
  344.0 5.0 %fusion.55 = f32[32,4096]{1,0:T(8,128)S(1)} fusion(bf16[1024,4096]{1,0:T(8,128)(2,1)} %get-tuple-element.171, bf16[32,1024]{1,0:T(8,128)(2,1)S(1)} %get-tuple-element.157, bf16[32]{0:T(256)(128)(2,1)S(1)} %get-tuple-element.142), kind=kOutput, calls=%fused_computation.24.clone.1 | convolution fusion | flops 268468224 | bytes 8978496 | tf_op jit(solution)/shard_map/while/body/eval_jaxpr/dot_general | solution.py:39
  351.2 5.0 %fusion.55 = f32[32,4096]{1,0:T(8,128)S(1)} fusion(bf16[1024,4096]{1,0:T(8,128)(2,1)} %get-tuple-element.171, bf16[32,1024]{1,0:T(8,128)(2,1)S(1)} %get-tuple-element.157, bf16[32]{0:T(256)(128)(2,1)S(1)} %get-tuple-element.142), kind=kOutput, calls=%fused_computation.24.clone.1 | convolution fusion | flops 268468224 | bytes 8978496 | tf_op jit(solution)/shard_map/while/body/eval_jaxpr/dot_general | solution.py:39
  358.4 5.0 %fusion.55 = f32[32,4096]{1,0:T(8,128)S(1)} fusion(bf16[1024,4096]{1,0:T(8,128)(2,1)} %get-tuple-element.171, bf16[32,1024]{1,0:T(8,128)(2,1)S(1)} %get-tuple-element.157, bf16[32]{0:T(256)(128)(2,1)S(1)} %get-tuple-element.142), kind=kOutput, calls=%fused_computation.24.clone.1 | convolution fusion | flops 268468224 | bytes 8978496 | tf_op jit(solution)/shard_map/while/body/eval_jaxpr/dot_general | solution.py:39
  365.6 5.0 %fusion.55 = f32[32,4096]{1,0:T(8,128)S(1)} fusion(bf16[1024,4096]{1,0:T(8,128)(2,1)} %get-tuple-element.171, bf16[32,1024]{1,0:T(8,128)(2,1)S(1)} %get-tuple-element.157, bf16[32]{0:T(256)(128)(2,1)S(1)} %get-tuple-element.142), kind=kOutput, calls=%fused_computation.24.clone.1 | convolution fusion | flops 268468224 | bytes 8978496 | tf_op jit(solution)/shard_map/while/body/eval_jaxpr/dot_general | solution.py:39
  372.8 5.0 %fusion.55 = f32[32,4096]{1,0:T(8,128)S(1)} fusion(bf16[1024,4096]{1,0:T(8,128)(2,1)} %get-tuple-element.171, bf16[32,1024]{1,0:T(8,128)(2,1)S(1)} %get-tuple-element.157, bf16[32]{0:T(256)(128)(2,1)S(1)} %get-tuple-element.142), kind=kOutput, calls=%fused_computation.24.clone.1 | convolution fusion | flops 268468224 | bytes 8978496 | tf_op jit(solution)/shard_map/while/body/eval_jaxpr/dot_general | solution.py:39
  395.2 28.5 %all_to_all.30 = bf16[32,2,16,1024]{3,1,2,0:T(2,128)(2,1)S(1)} all-to-all(bf16[32,2,16,1024]{3,1,2,0:T(2,128)(2,1)S(1)} %copy.48), channel_id=1, replica_groups=mesh['batch'=32,'head'=4] {'head'}, dimensions={0} | all-to-all | bytes 4194304 | tf_op jit(solution)/shard_map/all_to_all | solution.py:93
  424.4 8.3 %maximum_convert_fusion = bf16[8,128,1024]{2,1,0:T(8,128)(2,1)S(1)} fusion(bf16[8,128,1024]{2,1,0:T(8,128)(2,1)S(1)} %bitcast.88, bf16[8,1024,1024]{2,1,0:T(8,128)(2,1)} %param.25), kind=kOutput, calls=%fused_computation.31 | convolution fusion | flops 2149580800 | bytes 20971520 | tf_op jit(solution)/shard_map/prh,phk->prk/dot_general | solution.py:96
  434.7 6.6 %all_to_all.31 = bf16[4,2,2304]{2,1,0:T(2,128)(2,1)S(1)} all-to-all(bf16[4,2,2304]{2,1,0:T(2,128)(2,1)S(1)} %reshape.120), channel_id=1, replica_groups=mesh['batch'=32,'head'=4] {'head'}, dimensions={0} | all-to-all | bytes 73728 | tf_op jit(solution)/shard_map/all_to_all | solution.py:107
  (153 shorter events, 89.2 us)
Async XLA Ops:
  7.2 425.5 %copy-start = (bf16[8,512,18]{1,0,2:T(8,128)(2,1)S(1)}, bf16[8,512,18]{1,0,2:T(8,128)(2,1)}, u32[]{:S(2)}) copy-start(bf16[8,512,18]{1,0,2:T(8,128)(2,1)} %param.27) | copy-start | bytes 442372
  7.2 10.6 %copy-start.1 = (bf16[32,24,512]{2,1,0:T(8,128)(2,1)S(1)}, bf16[32,24,512]{2,1,0:T(8,128)(2,1)}, u32[]{:S(2)}) copy-start(bf16[32,24,512]{2,1,0:T(8,128)(2,1)} %param.15) | copy-start | bytes 2359300
  7.2 10.9 %copy-start.9 = (s32[32]{0:T(128)S(1)}, s32[32]{0:T(128)}, u32[]{:S(2)}) copy-start(s32[32]{0:T(128)} %param.18) | copy-start | bytes 388
  7.2 10.9 %copy-start.7 = (s32[32,1]{0,1:T(1,128)S(1)}, s32[32,1]{0,1:T(1,128)}, u32[]{:S(2)}) copy-start(s32[32,1]{0,1:T(1,128)} %param.20) | copy-start | bytes 388
  7.2 11.1 %copy-start.5 = (s32[32,24]{0,1:T(8,128)S(1)}, s32[32,24]{0,1:T(8,128)}, u32[]{:S(2)}) copy-start(s32[32,24]{0,1:T(8,128)} %param.19) | copy-start | bytes 9220
  7.2 11.1 %copy-start.4 = (bf16[32,1024]{1,0:T(8,128)(2,1)S(1)}, bf16[32,1024]{1,0:T(8,128)(2,1)}, u32[]{:S(2)}) copy-start(bf16[32,1024]{1,0:T(8,128)(2,1)} %param.16) | copy-start | bytes 196612
  7.2 11.1 %copy-start.3 = (bf16[32,1024]{1,0:T(8,128)(2,1)S(1)}, bf16[32,1024]{1,0:T(8,128)(2,1)}, u32[]{:S(2)}) copy-start(bf16[32,1024]{1,0:T(8,128)(2,1)} %param.17) | copy-start | bytes 196612
  7.2 90.3 %all-gather.3.cloned.1.call-start = ((), (), s32[]{:S(2)}) async-start(), calls=%async_computation.2 | async-start | bytes 4325376 | tf_op jit(solution)/shard_map/all_gather | solution.py:73
  16.9 185.2 %all-gather.5.cloned.1.call-start = ((), (), s32[]{:S(2)}) async-start(), calls=%async_computation.3 | async-start | bytes 8650752 | tf_op jit(solution)/shard_map/all_gather | solution.py:77
  202.1 12.1 %copy-start.2 = (f32[4,1024]{1,0:T(4,128)S(1)}, f32[4,1024]{1,0:T(4,128)}, u32[]{:S(2)}) copy-start(f32[4,1024]{1,0:T(4,128)} %param.24) | copy-start | bytes 49156
  424.4 8.7 %copy-start.8 = (bf16[8,512]{1,0:T(8,128)(2,1)S(1)}, bf16[8,512]{1,0:T(8,128)(2,1)}, u32[]{:S(2)}) copy-start(bf16[8,512]{1,0:T(8,128)(2,1)} %param.26) | copy-start | bytes 24580
  433.1 9.2 %copy-start.6 = (s32[32,16]{0,1:T(8,128)S(1)}, s32[32,16]{0,1:T(8,128)}, u32[]{:S(2)}) copy-start(s32[32,16]{0,1:T(8,128)} %param.21) | copy-start | bytes 6148
Sparse Core Ops, SparseCore 0:
  17.0 80.4 all-gather.2
  100.6 101.4 all-gather.4
where the time goes:
time: 454 us; the launch traced here: 451 us
  waiting for transfers between devices  144 us (32%)
  matrix products  138 us (30%)
  local copies, waits for them, and re-layouts  82.2 us (18%)
  blocking collectives  43 us (9%)
  other arithmetic  28.7 us (6%)
  between operations  14.3 us (3%)
    dot_general x24, matrix products, lstm_cell(): jnp.dot(full_h, w_flat, preferred_element_type=jnp.float32)  119 us
    all_gather x1, waiting for transfers between devices, shards(): lax.all_gather(w_in_rows, 'batch', axis=0, tiled=True)  79.2 us
    all_gather x1, waiting for transfers between devices, shards(): lax.all_gather(w_rec_rows, 'batch', axis=0, tiled=True)  65.1 us
    all_to_all x1, blocking collectives, shards(): lax.all_to_all(packed, 'head', split_axis=0, concat_axis=1, tiled=True)  28.5 us
    dynamic_slice x24, local copies, waits for them, and re-layouts, shards(): lax.scan(advance, (start_h, start_c.astype(jnp.float32)), (pre, keeps))  26 us
    dynamic_update_slice x24, other arithmetic, shards(): lax.scan(advance, (start_h, start_c.astype(jnp.float32)), (pre, keeps))  19 us
    unnamed x26, local copies, waits for them, and re-layouts  18.5 us
    reshape x1, local copies, waits for them, and re-layouts, shards(): jnp.dot(feat_flat, w_in_full, preferred_element_type=jnp.float32)  15.6 us
  transfers between devices with their start and end apart: 2, of which 2 were waited for; matrix products, arithmetic and copies ran while one was open for 9% of the time, Pallas kernels for 0%

commit v1 on v0

--- a/solution.py
+++ b/solution.py
@@ -1,18 +1,223 @@
 import jax
 import jax.numpy as jnp
 from jax import lax
+from jax.experimental import pallas as pl
+from jax.experimental.pallas import tpu as pltpu
 from jax.sharding import PartitionSpec as P
 
 ACTIONS = 18
 POLICIES = 32
 CAPP = 2
-
-
-def in_one_piece(arrays, axis, dim, along):
-    widths = [a.shape[along] for a in arrays]
-    both = jnp.concatenate(arrays, axis=along)
-    filled = lax.all_gather(both, axis, axis=dim, tiled=True)
-    return tuple(jnp.split(filled, [sum(widths[:k]) for k in range(1, len(widths))], axis=along))
+MESH = pl.DeviceIdType.MESH
+ORDERS = ("xyz", "yzx", "zxy")
+SENDS = 128
+F32 = jnp.float32
+BF16 = jnp.bfloat16
+
+
+def here():
+    b = lax.axis_index("batch")
+    h = lax.axis_index("head")
+    return {"x": b % 4, "y": b // 4 % 2 * 2 + h // 2, "z": b // 8, "c": h % 2}
+
+
+def device(at):
+    return (at["z"] * 8 + at["y"] // 2 * 4 + at["x"], at["y"] % 2 * 2 + at["c"])
+
+
+def shifted(at, axis, by):
+    return {**at, axis: (at[axis] + by + 4) % 4}
+
+
+def entry_barrier(me):
+    barrier = pltpu.get_barrier_semaphore()
+    other = {**me, "c": 1 - me["c"]}
+    peers = [shifted(me, a, d) for a in "xyz" for d in (1, -1, 2)]
+    peers += [other, {**other, "y": me["y"] + 1 - 2 * (me["y"] % 2)}]
+    for p in peers:
+        pl.semaphore_signal(barrier, inc=1, device_id=device(p), device_id_type=MESH)
+    pl.semaphore_wait(barrier, len(peers))
+
+
+class Copies:
+    def __init__(self, send_sem, recv_sem):
+        self.sems = (send_sem, recv_sem)
+        self.sent = []
+
+    def send(self, src, dst, to):
+        k = len(self.sent)
+        copy = pltpu.make_async_remote_copy(
+            src_ref=src,
+            dst_ref=dst,
+            send_sem=self.sems[0].at[k],
+            recv_sem=self.sems[1].at[k],
+            device_id=device(to),
+            device_id_type=MESH,
+        )
+        copy.start()
+        self.sent.append(copy)
+        return copy
+
+    def push(self, ref, to):
+        return self.send(ref, ref, to)
+
+
+def gather(me, shard, full, copies):
+    other = {**me, "c": 1 - me["c"]}
+    crossed = []
+
+    def region(part, at, free=None, half=None):
+        z, x = at["z"], at["x"]
+        y = (at["y"] // 2, at["y"] % 2)
+        if free == "y":
+            y = (slice(None) if half is None else half, slice(None))
+        elif free is not None:
+            span = slice(None) if half is None else pl.ds(2 * half, 2)
+            z, x = (span, x) if free == "z" else (z, span)
+        return full.at[me["c"], z, y[0], y[1], x, :, pl.ds(16 * part, 16), :]
+
+    def cross(ref):
+        crossed.append(copies.push(ref, other))
+
+    full[me["c"], me["z"], me["y"] // 2, me["y"] % 2, me["x"]] = shard[...]
+    first, line, third, relay = {}, {}, {}, {}
+    for d in (1, -1, 2):
+        for k, (a, b, c) in enumerate(ORDERS):
+            own = shard.at[:, pl.ds(16 * k, 16), :]
+            first[k, d] = copies.send(own, region(k, me), shifted(me, a, d))
+
+    def along_last(k, m, at):
+        a, b, c = ORDERS[k]
+        for d in (1, -1):
+            third[k, m, d] = copies.push(region(k, at, free=a), shifted(me, c, d))
+
+    for k, (a, b, c) in enumerate(ORDERS):
+        for d in (1, -1, 2):
+            first[k, d].wait_recv()
+        for d in (1, -1):
+            line[k, d] = copies.push(region(k, me, free=a), shifted(me, b, d))
+        along_last(k, 0, me)
+        cross(region(k, me, free=a))
+    for k, (a, b, c) in enumerate(ORDERS):
+        for m, d in ((1, 1), (2, -1)):
+            line[k, d].wait_recv()
+            at = shifted(me, b, -d)
+            relay[k, d] = copies.push(region(k, at, free=a, half=(1 - d) // 2), shifted(me, b, d))
+            along_last(k, m, at)
+            cross(region(k, at, free=a))
+    for k, (a, b, c) in enumerate(ORDERS):
+        for d in (1, -1):
+            relay[k, d].wait_recv()
+        at = shifted(me, b, 2)
+        along_last(k, 3, at)
+        cross(region(k, at, free=a))
+    relay = {}
+    offsets = (0, -1, 1, 2)
+    for m in range(4):
+        for k, (a, b, c) in enumerate(ORDERS):
+            for d in (1, -1):
+                third[k, m, d].wait_recv()
+                at = shifted(shifted(me, b, offsets[m]), c, -d)
+                relay[k, m, d] = copies.push(region(k, at, free=a, half=(1 - d) // 2), shifted(me, c, d))
+                cross(region(k, at, free=a))
+    for m in range(4):
+        for k, (a, b, c) in enumerate(ORDERS):
+            for d in (1, -1):
+                relay[k, m, d].wait_recv()
+            cross(region(k, shifted(shifted(me, b, offsets[m]), c, 2), free=a))
+    for copy in crossed:
+        copy.wait_recv()
+
+
+def sigmoid(v):
+    return 0.5 * jnp.tanh(0.5 * v) + 0.5
+
+
+def core_kernel(
+    shard, feat, state_h, state_c, valid, ends, bias, out, full, pre, even, odd, cell, keep, send_sem, recv_sem
+):
+    me = here()
+    steps, seqs = 24, 32
+    entry_barrier(me)
+    copies = Copies(send_sem, recv_sem)
+    alive = 1.0 - ends[...].astype(F32)
+    for t in range(steps):
+        keep[t] = jnp.broadcast_to(alive[:, t : t + 1], (seqs, 128))
+    keep[steps] = jnp.ones((seqs, 128), F32)
+    start = jnp.broadcast_to(valid[...].astype(F32), (seqs, 128)) * keep[0]
+    start = jnp.concatenate([start] * 8, axis=1)
+    even[...] = (state_h[...].astype(F32) * start).astype(BF16)
+    cell[...] = state_c[...].astype(F32) * start
+    gather(me, shard, full, copies)
+
+    @pl.loop(0, 4)
+    def _(hp):
+        for pair in range(2):
+            tiles = [
+                full[hp % 2, :, :, hp // 2, :, 2 * pair + g, 0:16, :].reshape(512, 256) for g in range(2)
+            ]
+            got = jnp.dot(feat[...], jnp.concatenate(tiles, axis=1), preferred_element_type=F32)
+            for g in range(2):
+                at = 2 * pair + g
+                pre[hp * 4 + at] = got[:, g * 256 : g * 256 + 256] + bias[hp, at : at + 1, :]
+
+    def step(t, src, dst, save):
+        h = src[...]
+        alive = keep[t + 1]
+        alive = jnp.concatenate([alive, alive], axis=1)
+        rows = pl.ds(pl.multiple_of(t * seqs, seqs), seqs)
+        for hp in range(4):
+            gate = []
+            for g in range(4):
+                w = full[hp % 2, :, :, hp // 2, :, g, 16:48, :].reshape(1024, 256)
+                gate.append(jnp.dot(h, w, preferred_element_type=F32) + pre[hp * 4 + g, rows, :])
+            cols = slice(hp * 256, hp * 256 + 256)
+            c = sigmoid(gate[1]) * cell[:, cols] + sigmoid(gate[0]) * jnp.tanh(gate[2])
+            new = sigmoid(gate[3]) * jnp.tanh(c)
+            cell[:, cols] = c * alive
+            dst[:, cols] = (new * alive).astype(BF16)
+            if save:
+                out[t - 8, :, cols] = new.astype(BF16)
+
+    def two(save):
+        def body(i, _):
+            step(2 * i, even, odd, save)
+            step(2 * i + 1, odd, even, save)
+            return 0
+
+        return body
+
+    lax.fori_loop(0, 4, two(False), 0)
+    lax.fori_loop(4, 12, two(True), 0)
+    for copy in copies.sent:
+        copy.wait_send()
+
+
+def recurrent_core(w_input, w_recur, features, state_h, state_c, valid, ends, lstm_bias):
+    shard = jnp.concatenate([w_input, w_recur], axis=0).transpose(1, 0, 2)
+    feat = features.transpose(1, 0, 2).reshape(-1, features.shape[2])
+    bias = lstm_bias.reshape(4, 4, 256).transpose(1, 0, 2)
+    vmem = pl.BlockSpec(memory_space=pltpu.VMEM)
+    return pl.pallas_call(
+        core_kernel,
+        out_shape=jax.ShapeDtypeStruct((16, 32, 1024), BF16),
+        in_specs=[vmem] * 7,
+        out_specs=vmem,
+        scratch_shapes=[
+            pltpu.VMEM((2, 4, 2, 2, 4, 4, 48, 256), BF16),
+            pltpu.VMEM((16, 768, 256), F32),
+            pltpu.VMEM((32, 1024), BF16),
+            pltpu.VMEM((32, 1024), BF16),
+            pltpu.VMEM((32, 1024), F32),
+            pltpu.VMEM((25, 32, 128), F32),
+            pltpu.SemaphoreType.DMA((SENDS,)),
+            pltpu.SemaphoreType.DMA((SENDS,)),
+        ],
+        compiler_params=pltpu.CompilerParams(
+            collective_id=0, has_side_effects=True, vmem_limit_bytes=48 * 2**20
+        ),
+        name="core",
+    )(shard, feat, state_h, state_c, valid[:, None], ends, bias)
 
 
 def slot_table(owners, per_source, capacity, policies):
@@ -29,21 +234,6 @@
     target = owners * (sources * capacity) + anchor * capacity + rank
     total = policies * sources * capacity
     return (jnp.arange(total, dtype=jnp.int32)[:, None] == target[None, :]).astype(jnp.bfloat16)
-
-
-def lstm_cell(pre_t, full_h, cell_state, keep_t, w_flat, bias, width):
-    full_h = full_h * keep_t[:, None].astype(jnp.bfloat16)
-    cell_state = cell_state * keep_t[:, None]
-    gates = (
-        pre_t
-        + jnp.dot(full_h, w_flat, preferred_element_type=jnp.float32).reshape(-1, 4, width)
-        + bias
-    )
-    cell_state = jax.nn.sigmoid(gates[:, 1]) * cell_state + jax.nn.sigmoid(gates[:, 0]) * jnp.tanh(
-        gates[:, 2]
-    )
-    new_h = (jax.nn.sigmoid(gates[:, 3]) * jnp.tanh(cell_state)).astype(jnp.bfloat16)
-    return (new_h, cell_state)
 
 
 def shards(
@@ -64,27 +254,7 @@
     seq_dev, steps, width_e = features.shape
     width_h = state_h.shape[1]
     learn = actions.shape[1]
-    burn = steps - learn
-    keep_start = valid.astype(jnp.bfloat16)[:, None]
-    start_h = state_h * keep_start
-    start_c = state_c * keep_start
-    w_in_rows, w_rec_rows = in_one_piece((w_input, w_recur), "head", 2, 0)
-    feat_flat = features.transpose(1, 0, 2).reshape(-1, width_e)
-    w_in_full = lax.all_gather(w_in_rows, "batch", axis=0, tiled=True).reshape(width_e, 4 * width_h)
-    pre = jnp.dot(feat_flat, w_in_full, preferred_element_type=jnp.float32).reshape(
-        steps, seq_dev, 4, width_h
-    )
-    w_flat = lax.all_gather(w_rec_rows, "batch", axis=0, tiled=True).reshape(width_h, 4 * width_h)
-    keeps = 1.0 - ends.astype(jnp.float32).T
-
-    def advance(carry, inputs):
-        full_h, cell_state = carry
-        pre_t, keep_t = inputs
-        new_h, cell_state = lstm_cell(pre_t, full_h, cell_state, keep_t, w_flat, lstm_bias, width_h)
-        return ((new_h, cell_state), new_h)
-
-    _, outputs = lax.scan(advance, (start_h, start_c.astype(jnp.float32)), (pre, keeps))
-    learned = outputs[burn:]
+    learned = recurrent_core(w_input, w_recur, features, state_h, state_c, valid, ends, lstm_bias)
     table = slot_table(policy[:, 0], seq_dev, CAPP, POLICIES)
     packed = jnp.einsum("ks,tsu->ktu", table, learned, preferred_element_type=jnp.float32).astype(
         jnp.bfloat16

time: 454 us -> 144 us (0.32)
  waiting for transfers between devices: 144 us -> 0 us
  matrix products: 138 us -> 10.8 us
  Pallas kernels: 0 us -> 80.7 us
  local copies, waits for them, and re-layouts: 82.2 us -> 16.4 us
  other arithmetic: 28.7 us -> 1.62 us
  between operations: 14.3 us -> 0.81 us
  blocking collectives: 43 us -> 33.3 us
    all_gather x2 -> x0, waiting for transfers between devices: 144 us -> none  [the longest x1 79.2 us: shards(): lax.all_gather(w_in_rows, 'batch', axis=0, tiled=True)]
    dot_general x25 -> x0, matrix products: 126 us -> none  [the longest x24 119 us: lstm_cell(): jnp.dot(full_h, w_flat, preferred_element_type=jnp.float32)]
    pallas_call x0 -> x1, Pallas kernels: none -> 80.7 us  [recurrent_core(): pl.pallas_call(core_kernel, out_shape=jax.ShapeDtypeStruct((16, 32, 1024)...]
    dynamic_slice x24 -> x0, local copies, waits for them, and re-layouts: 26 us -> none  [shards(): lax.scan(advance, (start_h, start_c.astype(jnp.float32)), (pre, keeps))]
    dynamic_update_slice x24 -> x0, other arithmetic: 19 us -> none  [shards(): lax.scan(advance, (start_h, start_c.astype(jnp.float32)), (pre, keeps))]
    reshape x1 -> x0, local copies, waits for them, and re-layouts: 15.6 us -> none  [shards(): jnp.dot(feat_flat, w_in_full, preferred_element_type=jnp.float32)]
    dot_general x1 -> x0, local copies, waits for them, and re-layouts: 12.7 us -> none  [shards(): jnp.dot(feat_flat, w_in_full, preferred_element_type=jnp.float32)]
    unnamed x26 -> x18, local copies, waits for them, and re-layouts: 18.5 us -> 6.47 us
  transfers between devices with their start and end apart: 2 -> 0, of which waited for: 2 -> 0; matrix products, arithmetic and copies ran while one was open for 9% -> 0% of each run, Pallas kernels for 0% -> 0%
where the time goes in v1:
time: 144 us
  Pallas kernels  80.7 us (56%)
  blocking collectives  33.3 us (23%)
  local copies, waits for them, and re-layouts  16.4 us (11%)
  matrix products  10.8 us (8%)
  other arithmetic  1.62 us (1%)
    pallas_call x1, Pallas kernels, recurrent_core(): pl.pallas_call(core_kernel, out_shape=jax.ShapeDtypeStruct((16, 32, 1024)...  80.7 us
    all_to_all x1, blocking collectives, shards(): lax.all_to_all(packed, 'head', split_axis=0, concat_axis=1, tiled=True)  26.7 us
    dot_general x1, matrix products, shards(): jnp.einsum('prh,phk->prk', rows, w_hidden, preferred_element_type=jnp.flo...  8.28 us
    all_to_all x1, blocking collectives, shards(): lax.all_to_all(q_local.astype(jnp.bfloat16), 'head', split_axis=1, concat...  6.58 us
    unnamed x18, local copies, waits for them, and re-layouts  6.47 us
    reshape x2, local copies, waits for them, and re-layouts, shards(): packed = packed.reshape(POLICIES, CAPP, learn, width_h)  6.01 us

profile of v1, /device:TPU:1, one launch (start us, length us, event | category | flops | bytes accessed | tf_op | source)
XLA Modules:
  0.0 143.5 jit_solution(6184272722952105666)
XLA Ops:
  0.6 0.0 copy-start
  0.7 0.9 convert_reduce_fusion
  1.6 0.7 multiply_add_fusion
  2.2 0.7 copy.51.valid
  3.0 0.8 copy.52.ends
  3.8 0.8 copy.48
  4.5 0.8 copy.49
  5.4 1.4 copy.50
  6.8 0.0 copy-start.1
  6.8 0.8 copy-done.1
  7.6 0.8 copy-done.2
  8.4 0.7 copy-done.3
  9.2 80.7 %core.1 = bf16[16,32,1024]{2,1,0:T(8,128)(2,1)S(1)} custom-call(bf16[4,48,256]{2,1,0:T(8,128)(2,1)S(1)} %maximum_bitcast_fusion.shard, bf16[768,512]{1,0:T(8,128)(2,1)S(1)} %bitcast.40, bf16[32,1024]{1,0:T(8,128)(2,1)S(1)} %copy-done.1, bf16[32,1024]{1,0:T(8,128)(2,1)S(1)} %copy-done.2, s32[32,1]{1,0:T(8,128)S(1)} %copy.51.valid, s32[32,24]{1,0:T(8,128)S(1)} %copy.52.ends, ...), custom_call_target="tpu_custom_call" | custom-call | tf_op jit(solution)/shard_map/core/pallas_call | solution.py:201
  89.8 0.8 convolution_convert_fusion
  90.7 2.2 %reshape.71 = bf16[32,2,16,1024]{3,1,0,2:T(2,128)(2,1)} reshape(bf16[64,16,1024]{2,0,1:T(8,128)(2,1)S(1)} %convolution_convert_fusion) | data formatting | bytes 4194304 | tf_op jit(solution)/shard_map/reshape | solution.py:262
  92.9 3.8 %copy.53 = bf16[32,2,16,1024]{3,1,2,0:T(2,128)(2,1)S(1)} copy(bf16[32,2,16,1024]{3,1,0,2:T(2,128)(2,1)} %reshape.71) | data formatting | bytes 4194304 | tf_op jit(solution)/shard_map/reshape | solution.py:262
  96.7 26.7 %all_to_all.30 = bf16[32,2,16,1024]{3,1,2,0:T(2,128)(2,1)S(1)} all-to-all(bf16[32,2,16,1024]{3,1,2,0:T(2,128)(2,1)S(1)} %copy.53), channel_id=1, replica_groups=mesh['batch'=32,'head'=4] {'head'}, dimensions={0} | all-to-all | bytes 4194304 | tf_op jit(solution)/shard_map/all_to_all | solution.py:263
  123.4 0.7 copy.54
  124.0 0.0 copy-start.5
  124.1 8.3 %maximum_convert_fusion = bf16[8,128,1024]{2,1,0:T(8,128)(2,1)S(1)} fusion(bf16[8,128,1024]{2,1,0:T(8,128)(2,1)S(1)} %bitcast.42, bf16[8,1024,1024]{2,1,0:T(8,128)(2,1)} %param.23), kind=kOutput, calls=%fused_computation | convolution fusion | flops 2149580800 | bytes 20971520 | tf_op jit(solution)/shard_map/prh,phk->prk/dot_general | solution.py:266
  132.3 0.0 copy-done.5
  132.4 0.4 fusion.2
  132.7 0.4 fusion.13
  133.2 0.2 reshape.77
  133.4 0.5 copy.57
  133.9 0.4 reshape.78
  134.4 6.6 %all_to_all.31 = bf16[4,2,2304]{2,1,0:T(2,128)(2,1)S(1)} all-to-all(bf16[4,2,2304]{2,1,0:T(2,128)(2,1)S(1)} %reshape.78), channel_id=1, replica_groups=mesh['batch'=32,'head'=4] {'head'}, dimensions={0} | all-to-all | bytes 73728 | tf_op jit(solution)/shard_map/all_to_all | solution.py:277
  140.9 0.6 reshape.79
  141.5 0.3 reshape.73
  141.8 0.1 copy.59
  142.0 0.9 select_reduce_fusion
  142.9 0.7 copy.60
  (11 shorter events, 0.1 us)
Async XLA Ops:
  0.6 132.1 %copy-start = (bf16[8,512,18]{1,0,2:T(8,128)(2,1)S(1)}, bf16[8,512,18]{1,0,2:T(8,128)(2,1)}, u32[]{:S(2)}) copy-start(bf16[8,512,18]{1,0,2:T(8,128)(2,1)} %param.25) | copy-start | bytes 442372
  6.8 0.8 copy-start.1
  7.6 0.8 copy-start.2
  8.4 0.7 copy-start.3
  124.0 8.3 %copy-start.5 = (bf16[8,512]{1,0:T(8,128)(2,1)S(1)}, bf16[8,512]{1,0:T(8,128)(2,1)}, u32[]{:S(2)}) copy-start(bf16[8,512]{1,0:T(8,128)(2,1)} %param.24) | copy-start | bytes 24580
  132.7 9.2 %copy-start.4 = (s32[32,16]{0,1:T(8,128)S(1)}, s32[32,16]{0,1:T(8,128)}, u32[]{:S(2)}) copy-start(s32[32,16]{0,1:T(8,128)} %param.19) | copy-start | bytes 6148

commit v2 on v1

v2 whole, which is shorter than its diff:
```python
import jax
import jax.numpy as jnp
from jax import lax
from jax.experimental import pallas as pl
from jax.experimental.pallas import tpu as pltpu
from jax.sharding import PartitionSpec as P

ACTIONS = 18
MESH = pl.DeviceIdType.MESH
ORDERS = ("xyz", "yzx", "zxy")
SENDS = 128
F32 = jnp.float32
BF16 = jnp.bfloat16


def here():
    b = lax.axis_index("batch")
    h = lax.axis_index("head")
    return {"x": b % 4, "y": b // 4 % 2 * 2 + h // 2, "z": b // 8, "c": h % 2}


def device(at):
    return (at["z"] * 8 + at["y"] // 2 * 4 + at["x"], at["y"] % 2 * 2 + at["c"])


def shifted(at, axis, by):
    return {**at, axis: (at[axis] + by + 4) % 4}


def entry_barrier(me):
    barrier = pltpu.get_barrier_semaphore()
    other = {**me, "c": 1 - me["c"]}
    peers = [shifted(me, a, d) for a in "xyz" for d in (1, -1, 2)]
    peers += [other, {**other, "y": me["y"] + 1 - 2 * (me["y"] % 2)}]
    for p in peers:
        pl.semaphore_signal(barrier, inc=1, device_id=device(p), device_id_type=MESH)
    pl.semaphore_wait(barrier, len(peers))


class Copies:
    def __init__(self, send_sem, recv_sem):
        self.sems = (send_sem, recv_sem)
        self.sent = []

    def send(self, src, dst, to):
        k = len(self.sent)
        copy = pltpu.make_async_remote_copy(
            src_ref=src,
            dst_ref=dst,
            send_sem=self.sems[0].at[k],
            recv_sem=self.sems[1].at[k],
            device_id=device(to),
            device_id_type=MESH,
        )
        copy.start()
        self.sent.append(copy)
        return copy

    def push(self, ref, to):
        return self.send(ref, ref, to)


def gather(me, shard, full, copies, meanwhile):
    other = {**me, "c": 1 - me["c"]}
    crossed = []

    def region(part, at, free=None, half=None):
        z, x = at["z"], at["x"]
        y = (at["y"] // 2, at["y"] % 2)
        if free == "y":
            y = (slice(None) if half is None else half, slice(None))
        elif free is not None:
            span = slice(None) if half is None else pl.ds(2 * half, 2)
            z, x = (span, x) if free == "z" else (z, span)
        return full.at[me["c"], z, y[0], y[1], x, :, pl.ds(16 * part, 16), :]

    def cross(ref):
        crossed.append(copies.push(ref, other))

    full[me["c"], me["z"], me["y"] // 2, me["y"] % 2, me["x"]] = shard[...]
    first, line, third, relay = {}, {}, {}, {}
    for d in (1, -1, 2):
        for k, (a, b, c) in enumerate(ORDERS):
            own = shard.at[:, pl.ds(16 * k, 16), :]
            first[k, d] = copies.send(own, region(k, me), shifted(me, a, d))
    meanwhile()

    def along_last(k, m, at):
        a, b, c = ORDERS[k]
        for d in (1, -1):
            third[k, m, d] = copies.push(region(k, at, free=a), shifted(me, c, d))

    for k, (a, b, c) in enumerate(ORDERS):
        for d in (1, -1, 2):
            first[k, d].wait_recv()
        for d in (1, -1):
            line[k, d] = copies.push(region(k, me, free=a), shifted(me, b, d))
        along_last(k, 0, me)
        cross(region(k, me, free=a))
    for k, (a, b, c) in enumerate(ORDERS):
        for m, d in ((1, 1), (2, -1)):
            line[k, d].wait_recv()
            at = shifted(me, b, -d)
            relay[k, d] = copies.push(region(k, at, free=a, half=(1 - d) // 2), shifted(me, b, d))
            along_last(k, m, at)
            cross(region(k, at, free=a))
    for k, (a, b, c) in enumerate(ORDERS):
        for d in (1, -1):
            relay[k, d].wait_recv()
        at = shifted(me, b, 2)
        along_last(k, 3, at)
        cross(region(k, at, free=a))
    relay = {}
    offsets = (0, -1, 1, 2)
    for m in range(4):
        for k, (a, b, c) in enumerate(ORDERS):
            for d in (1, -1):
                third[k, m, d].wait_recv()
                at = shifted(shifted(me, b, offsets[m]), c, -d)
                relay[k, m, d] = copies.push(region(k, at, free=a, half=(1 - d) // 2), shifted(me, c, d))
                cross(region(k, at, free=a))
    for m in range(4):
        for k, (a, b, c) in enumerate(ORDERS):
            for d in (1, -1):
                relay[k, m, d].wait_recv()
            cross(region(k, shifted(shifted(me, b, offsets[m]), c, 2), free=a))
    for copy in crossed:
        copy.wait_recv()


def sigmoid(v):
    return 0.5 * jnp.tanh(0.5 * v) + 0.5


def iota(shape, dim):
    return lax.broadcasted_iota(jnp.int32, shape, dim)


def ones_where(mask, dtype):
    return jnp.where(mask, 1.0, 0.0).astype(dtype)


def prepare(table, wv, wa, head, keep, info, value_w, adv_w, spread, lane_group, chosen):
    ends = table[:, 0:24].astype(F32)
    for t in range(24):
        keep[t] = jnp.broadcast_to(1.0 - ends[:, t : t + 1], (32, 128))
    keep[24] = jnp.ones((32, 128), F32)
    policy = jnp.broadcast_to(table[:, 40:41], (32, 256)).astype(F32)
    seq = iota((32, 256), 1) & 31
    row = iota((32, 256), 0)
    across = jnp.sum(jnp.where(row == seq, policy, 0.0), axis=0, keepdims=True)
    same = policy == across
    rank_across = jnp.sum(ones_where(same & (row < seq), F32), axis=0, keepdims=True)
    info[head] = jnp.concatenate(
        [jnp.broadcast_to(across, (8, 256)), jnp.broadcast_to(rank_across, (8, 256))], axis=0
    )

    def finish():
        lane = iota((32, 128), 1)
        earlier = same[:, 0:128] & (lane < row[:, 0:128])
        rank = jnp.sum(ones_where(earlier, F32), axis=1, keepdims=True)
        number = table[:, 40:41]
        base = (number >> 2).astype(F32) * 32.0 + rank * 8.0
        group = (number & 3).astype(F32)
        each = ones_where((iota((512, 32), 0) >> 4) == iota((512, 32), 1), BF16)
        place = iota((512, 128), 0) & 15

        def per_row(column):
            wide = jnp.broadcast_to(column, (32, 128)).astype(BF16)
            return jnp.dot(each, wide, preferred_element_type=F32)

        slot = per_row(base) + ((place >> 3) * 16 + (place & 7)).astype(F32)
        slot = jnp.concatenate([slot, slot], axis=1)
        spread[...] = ones_where(slot == iota((512, 256), 1).astype(F32), BF16)
        lanes = iota((512, 128), 1)
        lane_group[...] = ones_where((lanes >> 5).astype(F32) == per_row(group), F32)
        taken = jnp.dot(each, table[:, 24:40].astype(F32).astype(BF16), preferred_element_type=F32)
        at = iota((512, 16), 1) == (iota((512, 16), 0) & 15)
        taken = jnp.sum(jnp.where(at, taken, 0.0), axis=1, keepdims=True)
        chosen[...] = ones_where(jnp.broadcast_to(taken, (512, 128)) == lanes.astype(F32), F32)
        adv_w[...] = jnp.zeros(adv_w.shape, BF16)
        adv_w[:, :, 0:ACTIONS] = wa[...]
        for p in range(8):
            line = wv[p : p + 1, :].astype(F32)
            value_w[p] = jnp.broadcast_to(line, (128, 512)).T.astype(BF16)

    return finish


def core_kernel(
    shard,
    table,
    bias,
    wv,
    wa,
    feat_hbm,
    state_h,
    state_c,
    wh_hbm,
    q_out,
    taken_out,
    full,
    pre,
    even,
    odd,
    cell,
    keep,
    feat,
    hidden_w,
    learned,
    packed,
    info,
    pick,
    value_w,
    adv_w,
    spread,
    lane_group,
    chosen,
    answers,
    replies,
    local_sem,
    send_sem,
    recv_sem,
    route_send,
    route_recv,
):
    me = here()
    seqs = 32
    head = me["y"] % 2 * 2 + me["c"]
    other = {**me, "c": 1 - me["c"]}
    facing = {**me, "y": me["y"] + 1 - 2 * (me["y"] % 2)}
    across = {**facing, "c": 1 - me["c"]}
    head_of = lambda at: at["y"] % 2 * 2 + at["c"]
    loads = [pltpu.make_async_copy(feat_hbm, feat, local_sem.at[8])]
    loads[0].start()
    entry_barrier(me)
    copies = Copies(send_sem, recv_sem)
    told = []

    def meanwhile():
        for p in range(8):
            loads.append(pltpu.make_async_copy(wh_hbm.at[p], hidden_w.at[p], local_sem.at[p]))
            loads[-1].start()
        rest = prepare(table, wv, wa, head, keep, info, value_w, adv_w, spread, lane_group, chosen)
        start = jnp.broadcast_to(table[:, 41:42].astype(F32), (seqs, 128)) * keep[0]
        start = jnp.concatenate([start] * 8, axis=1)
        even[...] = (state_h[...].astype(F32) * start).astype(BF16)
        cell[...] = state_c[...].astype(F32) * start
        rest()
        for to in (other, facing, across):
            told.append(copies.push(info.at[head], to))

    gather(me, shard, full, copies, meanwhile)
    loads[0].wait()
    for copy in told:
        copy.wait_recv()
    lane = iota((128, 256), 1)
    row = iota((128, 256), 0)
    step_at = (lane >> 5) == (row & 7)
    for s in range(4):
        mine = info[s, 0:1, :] == ((row >> 4) + 8 * head).astype(F32)
        cap = info[s, 8:9, :] == ((row >> 3) & 1).astype(F32)
        pick[s] = ones_where(mine & cap & step_at, BF16)

    for hp in range(4):
        for pair in range(2):
            tiles = [
                full[hp % 2, :, :, hp // 2, :, 2 * pair + g, 0:16, :].reshape(512, 256) for g in range(2)
            ]
            got = jnp.dot(feat[...], jnp.concatenate(tiles, axis=1), preferred_element_type=F32)
            for g in range(2):
                at = 2 * pair + g
                line = bias[at : at + 1, hp * 256 : hp * 256 + 256]
                pre[hp * 4 + at] = got[:, g * 256 : g * 256 + 256] + line

    def step(t, src, dst, save):
        h = src[...]
        alive = keep[t + 1]
        alive = jnp.concatenate([alive, alive], axis=1)
        rows = pl.ds(pl.multiple_of(t * seqs, seqs), seqs)
        for hp in range(4):
            gate = []
            for g in range(4):
                w = full[hp % 2, :, :, hp // 2, :, g, 16:48, :].reshape(1024, 256)
                gate.append(jnp.dot(h, w, preferred_element_type=F32) + pre[hp * 4 + g, rows, :])
            cols = slice(hp * 256, hp * 256 + 256)
            c = sigmoid(gate[1]) * cell[:, cols] + sigmoid(gate[0]) * jnp.tanh(gate[2])
            new = sigmoid(gate[3]) * jnp.tanh(c)
            cell[:, cols] = c * alive
            dst[:, cols] = (new * alive).astype(BF16)
            if save:
                learned[head, t - 8, :, cols] = new.astype(BF16)

    def route(kind, i, owner, to):
        ref = learned.at[head_of(owner), i]
        return pltpu.make_async_remote_copy(
            src_ref=ref,
            dst_ref=ref,
            send_sem=route_send.at[kind, i],
            recv_sem=route_recv.at[kind, i],
            device_id=device(to),
            device_id_type=MESH,
        )

    def send_out(i):
        route(1, i, me, facing).start()
        route(0, i, me, other).start()

    def hand_on(i):
        route(1, i, me, facing).wait_recv()
        route(2, i, facing, other).start()

    def burn(i, _):
        step(2 * i, even, odd, False)
        step(2 * i + 1, odd, even, False)
        return 0

    lag = 4

    def learn(i, _):
        @pl.when(i > 0)
        def _():
            send_out(2 * i - 1)

        @pl.when(2 * i >= lag)
        def _():
            hand_on(2 * i - lag)
            hand_on(2 * i - lag + 1)

        step(2 * i + 8, even, odd, True)
        send_out(2 * i)
        step(2 * i + 9, odd, even, True)
        return 0

    lax.fori_loop(0, 4, burn, 0)
    lax.fori_loop(0, 8, learn, 0)
    send_out(15)

    def pack(s, half):
        rows = learned[s, 8 * half : 8 * half + 8].reshape(256, 1024)
        got = jnp.dot(pick[s], rows, preferred_element_type=F32).astype(BF16)
        packed[:, (2 * s + half) * 16 : (2 * s + half) * 16 + 16, :] = got.reshape(8, 16, 1024)

    for i in range(16 - lag, 16):
        hand_on(i)
    for i in range(16):
        route(0, i, me, other).wait_recv()
        route(2, i, facing, other).wait_recv()
    for s in range(4):
        for half in range(2):
            pack(s, half)
    for load in loads[1:]:
        load.wait()
    valid_lane = iota((128, 128), 1) < ACTIONS
    for quad in range(2):
        total = None
        for j in range(4):
            p = 4 * quad + j
            mid = jnp.dot(packed[p], hidden_w[p], preferred_element_type=F32)
            mid = jnp.maximum(mid, 0.0).astype(BF16)
            value = jnp.dot(mid[:, 0:512], value_w[p], preferred_element_type=F32)
            adv = jnp.dot(mid[:, 512:1024], adv_w[p], preferred_element_type=F32)
            q = value + adv - jnp.sum(adv, axis=1, keepdims=True) * (1.0 / ACTIONS)
            q = jnp.where(valid_lane, q, 0.0)
            if j:
                q = pltpu.roll(q, 32 * j, 1)
            total = q if total is None else total + q
        for s in range(4):
            answers[s, 32 * quad : 32 * quad + 32, :] = total[32 * s : 32 * s + 32].astype(BF16)
    replies[head] = answers[head]
    back = []
    for to in (across, facing, other):
        back.append(copies.send(answers.at[head_of(to)], replies.at[head], to))
    for copy in back:
        copy.wait_recv()
    found = jnp.dot(spread[...], replies[...].reshape(256, 128), preferred_element_type=F32)
    found = (found * lane_group[...]).astype(BF16)
    fold = ones_where((iota((128, 128), 0) & 31) == iota((128, 128), 1), BF16)
    q = jnp.dot(found, fold, preferred_element_type=F32)
    q_out[...] = q.reshape(32, 16, 128)[:, :, 0:ACTIONS]
    picked = jnp.sum(q * chosen[...], axis=1, keepdims=True)
    at = iota((512, 16), 1) == (iota((512, 16), 0) & 15)
    picked = jnp.where(at, jnp.broadcast_to(picked, (512, 16)), 0.0).astype(BF16)
    collect = ones_where((iota((32, 512), 1) >> 4) == iota((32, 512), 0), BF16)
    taken_out[...] = jnp.dot(collect, picked, preferred_element_type=F32)
    for i in range(16):
        route(0, i, me, other).wait_send()
        route(1, i, me, facing).wait_send()
        route(2, i, facing, other).wait_send()
    for copy in copies.sent:
        copy.wait_send()


def shards(
    features,
    state_h,
    state_c,
    valid,
    ends,
    policy,
    actions,
    w_input,
    w_recur,
    lstm_bias,
    w_hidden,
    w_value,
    w_advantage,
):
    shard = jnp.concatenate([w_input, w_recur], axis=0).transpose(1, 0, 2)
    feat = features.transpose(1, 0, 2).reshape(-1, features.shape[2])
    table = jnp.concatenate([ends, actions, policy, valid[:, None]], axis=1)
    vmem = pl.BlockSpec(memory_space=pltpu.VMEM)
    hbm = pl.BlockSpec(memory_space=pl.ANY)
    dma = pltpu.SemaphoreType.DMA
    return pl.pallas_call(
        core_kernel,
        out_shape=(
            jax.ShapeDtypeStruct((32, 16, ACTIONS), F32),
            jax.ShapeDtypeStruct((32, 16), F32),
        ),
        in_specs=[vmem] * 5 + [hbm] + [vmem] * 2 + [hbm],
        out_specs=(vmem, vmem),
        scratch_shapes=[
            pltpu.VMEM((2, 4, 2, 2, 4, 4, 48, 256), BF16),
            pltpu.VMEM((16, 768, 256), F32),
            pltpu.VMEM((32, 1024), BF16),
            pltpu.VMEM((32, 1024), BF16),
            pltpu.VMEM((32, 1024), F32),
            pltpu.VMEM((25, 32, 128), F32),
            pltpu.VMEM((768, 512), BF16),
            pltpu.VMEM((8, 1024, 1024), BF16),
            pltpu.VMEM((4, 16, 32, 1024), BF16),
            pltpu.VMEM((8, 128, 1024), BF16),
            pltpu.VMEM((4, 16, 256), F32),
            pltpu.VMEM((4, 128, 256), BF16),
            pltpu.VMEM((8, 512, 128), BF16),
            pltpu.VMEM((8, 512, 128), BF16),
            pltpu.VMEM((512, 256), BF16),
            pltpu.VMEM((512, 128), F32),
            pltpu.VMEM((512, 128), F32),
            pltpu.VMEM((4, 64, 128), BF16),
            pltpu.VMEM((4, 64, 128), BF16),
            dma((9,)),
            dma((SENDS,)),
            dma((SENDS,)),
            dma((3, 16)),
            dma((3, 16)),
        ],
        compiler_params=pltpu.CompilerParams(
            collective_id=0, has_side_effects=True, vmem_limit_bytes=60 * 2**20
        ),
        name="core",
    )(shard, table, lstm_bias, w_value, w_advantage, feat, state_h, state_c, w_hidden)


def solution(mesh):
    return jax.shard_map(
        shards,
        mesh=mesh,
        in_specs=(
            P(("batch", "head"), None, None),
            P(("batch", "head"), None),
            P(("batch", "head"), None),
            P(("batch", "head")),
            P(("batch", "head"), None),
            P(("batch", "head"), None),
            P(("batch", "head"), None),
            P("batch", None, "head"),
            P("batch", None, "head"),
            P(),
            P("head", None, None),
            P("head", None),
            P("head", None, None),
        ),
        out_specs=(P(("batch", "head"), None, None), P(("batch", "head"), None)),
        check_vma=False,
    )
```

time: 144 us -> 112 us (0.78)
  blocking collectives: 33.3 us -> 0 us
  Pallas kernels: 80.7 us -> 96.6 us
  matrix products: 10.8 us -> 0 us
  local copies, waits for them, and re-layouts: 16.4 us -> 12.4 us
    all_to_all x2 -> x0, blocking collectives: 33.3 us -> none  [the longest x1 26.7 us: shards(): lax.all_to_all(packed, 'head', split_axis=0, concat_axis=1, tiled=True)]
    pallas_call x1, Pallas kernels: 80.7 us -> 96.6 us  [shards(): pl.pallas_call(core_kernel, out_shape=(jax.ShapeDtypeStruct((32, 16, ACTI...]
    dot_general x5 -> x0, matrix products: 10.8 us -> none  [the longest x1 8.28 us: shards(): jnp.einsum('prh,phk->prk', rows, w_hidden, preferred_element_type=jnp.flo...]
    reshape x3 -> x0, local copies, waits for them, and re-layouts: 6.26 us -> none  [the longest x2 6.01 us: shards(): packed = packed.reshape(POLICIES, CAPP, learn, width_h)]
    pallas_call x0 -> x2, local copies, waits for them, and re-layouts: none -> 3.18 us  [shards(): pl.pallas_call(core_kernel, out_shape=(jax.ShapeDtypeStruct((32, 16, ACTI...]
    unnamed x18 -> x6, local copies, waits for them, and re-layouts: 6.47 us -> 6.22 us
where the time goes in v2:
time: 112 us; the launch traced here: 111 us
  Pallas kernels  96.6 us (86%)
  local copies, waits for them, and re-layouts  12.4 us (11%)
  other arithmetic  1.34 us (1%)
    pallas_call x1, Pallas kernels, shards(): pl.pallas_call(core_kernel, out_shape=(jax.ShapeDtypeStruct((32, 16, ACTI...  96.6 us
    unnamed x6, local copies, waits for them, and re-layouts  6.22 us
    pallas_call x2, local copies, waits for them, and re-layouts, shards(): pl.pallas_call(core_kernel, out_shape=(jax.ShapeDtypeStruct((32, 16, ACTI...  3.18 us
    transpose x1, local copies, waits for them, and re-layouts, shards(): feat = features.transpose(1, 0, 2).reshape(-1, features.shape[2])  2.29 us

profile of v2, /device:TPU:1, one launch (start us, length us, event | category | flops | bytes accessed | tf_op | source)
XLA Modules:
  0.0 111.0 jit_solution(1199440194356337043)
XLA Ops:
  0.6 0.7 copy.20
  1.4 0.8 copy.17
  2.1 0.7 copy.19
  2.9 0.8 copy.18
  3.7 0.7 pad_add_fusion.table
  4.3 0.8 copy.15
  5.1 0.8 copy.16
  6.0 0.6 maximum_bitcast_fusion.shard
  6.6 2.3 %copy.21 = bf16[24,32,512]{2,1,0:T(8,128)(2,1)} copy(bf16[24,32,512]{2,0,1:T(8,128)(2,1)} %bitcast.6) | data formatting | bytes 1572864 | tf_op jit(solution)/shard_map/transpose | solution.py:410
  8.9 2.3 %copy.22.wa = bf16[8,512,18]{2,1,0:T(8,128)(2,1)} copy(bf16[8,512,18]{1,0,2:T(8,128)(2,1)} %param.25) | data formatting | bytes 294912 | tf_op args[12]
  11.2 96.6 %core.1 = (f32[32,16,18]{2,1,0:T(8,128)}, f32[32,16]{1,0:T(8,128)}) custom-call(bf16[4,48,256]{2,1,0:T(8,128)(2,1)} %maximum_bitcast_fusion.shard, s32[32,42]{1,0:T(8,128)} %pad_add_fusion.table, f32[4,1024]{1,0:T(4,128)} %bias.1, bf16[8,512]{1,0:T(8,128)(2,1)} %wv.1, bf16[8,512,18]{2,1,0:T(8,128)(2,1)} %copy.22.wa, bf16[768,512]{1,0:T(8,128)(2,1)} %bitcast.5, ...), custom_call_target="tpu_custom_call" | custom-call | tf_op jit(solution)/shard_map/core/pallas_call | solution.py:415
  107.9 1.8 %copy.23 = f32[32,16,18]{0,1,2:T(8,128)} copy(f32[32,16,18]{2,1,0:T(8,128)} %get-tuple-element.2) | data formatting | bytes 73728 | tf_op jit(solution)/shard_map/core/pallas_call | solution.py:415
  109.6 1.4 %copy.24 = f32[32,16]{0,1:T(8,128)} copy(f32[32,16]{1,0:T(8,128)} %get-tuple-element.3) | data formatting | bytes 4096 | tf_op jit(solution)/shard_map/core/pallas_call | solution.py:415

commit v3 on v2

v3 whole, which is shorter than its diff:
```python
import jax
import jax.numpy as jnp
from jax import lax
from jax.experimental import pallas as pl
from jax.experimental.pallas import tpu as pltpu
from jax.sharding import PartitionSpec as P

ACTIONS = 18
MESH = pl.DeviceIdType.MESH
ORDERS = ("xyz", "yzx", "zxy")
SENDS = 176
F32 = jnp.float32
BF16 = jnp.bfloat16


def here():
    b = lax.axis_index("batch")
    h = lax.axis_index("head")
    return {"x": b % 4, "y": b // 4 % 2 * 2 + h // 2, "z": b // 8, "c": h % 2}


def device(at):
    return (at["z"] * 8 + at["y"] // 2 * 4 + at["x"], at["y"] % 2 * 2 + at["c"])


def shifted(at, axis, by):
    return {**at, axis: (at[axis] + by + 4) % 4}


def entry_barrier(me):
    barrier = pltpu.get_barrier_semaphore()
    other = {**me, "c": 1 - me["c"]}
    peers = [shifted(me, a, d) for a in "xyz" for d in (1, -1, 2)]
    peers += [other, {**other, "y": me["y"] + 1 - 2 * (me["y"] % 2)}]
    for p in peers:
        pl.semaphore_signal(barrier, inc=1, device_id=device(p), device_id_type=MESH)
    pl.semaphore_wait(barrier, len(peers))


class Copies:
    def __init__(self, send_sem, recv_sem):
        self.sems = (send_sem, recv_sem)
        self.sent = []

    def send(self, src, dst, to):
        k = len(self.sent)
        copy = pltpu.make_async_remote_copy(
            src_ref=src,
            dst_ref=dst,
            send_sem=self.sems[0].at[k],
            recv_sem=self.sems[1].at[k],
            device_id=device(to),
            device_id_type=MESH,
        )
        copy.start()
        self.sent.append(copy)
        return copy

    def push(self, ref, to):
        return self.send(ref, ref, to)


def gather(me, shard, full, copies, meanwhile):
    other = {**me, "c": 1 - me["c"]}
    crossed = []

    def region(part, at, free=None, half=None):
        z, x = at["z"], at["x"]
        y = (at["y"] // 2, at["y"] % 2)
        if free == "y":
            y = (slice(None) if half is None else half, slice(None))
        elif free is not None:
            span = slice(None) if half is None else pl.ds(2 * half, 2)
            z, x = (span, x) if free == "z" else (z, span)
        return full.at[me["c"], z, y[0], y[1], x, :, pl.ds(16 * part, 16), :]

    def cross(ref):
        crossed.append(copies.push(ref, other))

    def own(k):
        return shard.at[:, pl.ds(16 * k, 16), :]

    first, relay = {}, {}
    line = {(k, d): [] for k in range(3) for d in (1, -1)}
    third = {(k, m, d): [] for k in range(3) for m in range(4) for d in (1, -1)}
    for d in (1, -1, 2):
        for k, (a, b, c) in enumerate(ORDERS):
            first[k, d] = copies.send(own(k), region(k, me), shifted(me, a, d))

    def along_both(k, at, src):
        a, b, c = ORDERS[k]
        for d in (1, -1):
            line[k, d].append(copies.send(src, region(k, at), shifted(me, b, d)))
        for d in (1, -1):
            third[k, 0, d].append(copies.send(src, region(k, at), shifted(me, c, d)))

    def along_last(k, m, at):
        a, b, c = ORDERS[k]
        for d in (1, -1):
            third[k, m, d].append(copies.push(region(k, at, free=a), shifted(me, c, d)))

    for k in range(3):
        along_both(k, me, own(k))
    full[me["c"], me["z"], me["y"] // 2, me["y"] % 2, me["x"]] = shard[...]
    meanwhile()
    for d in (1, -1, 2):
        for k, (a, b, c) in enumerate(ORDERS):
            first[k, d].wait_recv()
            at = shifted(me, a, -d)
            along_both(k, at, region(k, at))
    for k, (a, b, c) in enumerate(ORDERS):
        cross(region(k, me, free=a))
    for k, (a, b, c) in enumerate(ORDERS):
        for m, d in ((1, 1), (2, -1)):
            for copy in line[k, d]:
                copy.wait_recv()
            at = shifted(me, b, -d)
            relay[k, d] = copies.push(region(k, at, free=a, half=(1 - d) // 2), shifted(me, b, d))
            along_last(k, m, at)
            cross(region(k, at, free=a))
    for k, (a, b, c) in enumerate(ORDERS):
        for d in (1, -1):
            relay[k, d].wait_recv()
        at = shifted(me, b, 2)
        along_last(k, 3, at)
        cross(region(k, at, free=a))
    relay = {}
    offsets = (0, -1, 1, 2)
    for m in range(4):
        for k, (a, b, c) in enumerate(ORDERS):
            for d in (1, -1):
                for copy in third[k, m, d]:
                    copy.wait_recv()
                at = shifted(shifted(me, b, offsets[m]), c, -d)
                relay[k, m, d] = copies.push(region(k, at, free=a, half=(1 - d) // 2), shifted(me, c, d))
                cross(region(k, at, free=a))
    for m in range(4):
        for k, (a, b, c) in enumerate(ORDERS):
            for d in (1, -1):
                relay[k, m, d].wait_recv()
            cross(region(k, shifted(shifted(me, b, offsets[m]), c, 2), free=a))
    for copy in crossed:
        copy.wait_recv()


def sigmoid(v):
    return 0.5 * jnp.tanh(0.5 * v) + 0.5


def iota(shape, dim):
    return lax.broadcasted_iota(jnp.int32, shape, dim)


def ones_where(mask, dtype):
    return jnp.where(mask, 1.0, 0.0).astype(dtype)


def prepare(ends, actions, policy, valid, small, wv, wa, wide, head, keep, info, value_w, adv_w, spread, group):
    small[...] = jnp.zeros((128, 128), F32)
    small[0:24, 0:32] = ends[...].astype(F32)
    small[24:40, 0:32] = actions[...].astype(F32)
    small[40:41, 0:32] = policy[...].astype(F32)
    small[41:42, 0:32] = valid[...].astype(F32)
    by_seq = small[...].T
    for t in range(24):
        keep[t] = jnp.broadcast_to(1.0 - by_seq[0:32, t : t + 1], (32, 128))
    keep[24] = jnp.ones((32, 128), F32)
    rows = small[24:48, :]
    rows = rows + pltpu.roll(rows, 32, 1) + pltpu.roll(rows, 64, 1) + pltpu.roll(rows, 96, 1)
    across = rows[16:17, :]
    same = jnp.broadcast_to(by_seq[0:32, 40:41], (32, 128)) == across
    earlier = iota((32, 128), 0) < (iota((32, 128), 1) & 31)
    rank = jnp.sum(ones_where(same & earlier, F32), axis=0, keepdims=True)
    info[head] = jnp.concatenate(
        [jnp.broadcast_to(jnp.concatenate([v, v], axis=1), (8, 256)) for v in (across, rank)], axis=0
    )
    start = jnp.broadcast_to(by_seq[0:32, 41:42], (32, 128)) * keep[0]

    def finish():
        lane = iota((1, 512), 1)
        step = lane >> 5
        number = jnp.concatenate([across] * 4, axis=1).astype(jnp.int32)
        slot = (number >> 2) * 32 + (step >> 3) * 16 + (step & 7)
        slot = slot + jnp.concatenate([rank] * 4, axis=1).astype(jnp.int32) * 8
        spread[...] = ones_where(iota((256, 512), 0) == slot, BF16)
        group[...] = ones_where((iota((128, 512), 0) >> 5) == (number & 3), F32)
        picks = jnp.concatenate([rows[0:16, :]] * 4, axis=1)
        on = iota((16, 512), 0) == (iota((16, 512), 1) >> 5)
        for p in range(8):
            line = wv[p : p + 1, :].astype(F32)
            value_w[p] = jnp.broadcast_to(line, (128, 512)).T.astype(BF16)
        wide[...] = jnp.zeros((1024, 128), F32)
        for a in range(ACTIONS):
            line = wa[a].astype(F32)
            for col in range(4):
                wide[pl.ds(256 * col + a, 8, stride=32), :] = line[:, 128 * col : 128 * col + 128]
        for p in range(8):
            part = [wide[256 * col + 32 * p : 256 * col + 32 * p + 32, :] for col in range(4)]
            part = jnp.concatenate([jnp.concatenate(part, axis=1), jnp.zeros((96, 512), F32)], axis=0)
            adv_w[p] = part.T.astype(BF16)
        return jnp.sum(jnp.where(on, picks, 0.0), axis=0, keepdims=True)

    return start, finish


def core_kernel(
    w_in,
    w_rec,
    ends,
    actions,
    policy,
    valid,
    bias,
    wv,
    wa,
    state_h,
    state_c,
    feat_hbm,
    wh_hbm,
    q_out,
    taken_out,
    shard,
    full,
    pre,
    even,
    odd,
    cell,
    keep,
    raw,
    feat,
    hidden_w,
    learned,
    packed,
    small,
    wide,
    info,
    pick,
    value_w,
    adv_w,
    spread,
    group,
    act,
    answers,
    replies,
    local_sem,
    send_sem,
    recv_sem,
    route_send,
    route_recv,
):
    me = here()
    seqs = 32
    head = me["y"] % 2 * 2 + me["c"]
    other = {**me, "c": 1 - me["c"]}
    facing = {**me, "y": me["y"] + 1 - 2 * (me["y"] % 2)}
    diagonal = {**facing, "c": 1 - me["c"]}
    head_of = lambda at: at["y"] % 2 * 2 + at["c"]
    loads = [pltpu.make_async_copy(feat_hbm, raw, local_sem.at[8])]
    loads[0].start()
    for g in range(4):
        shard[g, 0:16, :] = w_in[:, g, :]
        shard[g, 16:48, :] = w_rec[:, g, :]
    entry_barrier(me)
    copies = Copies(send_sem, recv_sem)
    told = []

    def meanwhile():
        for p in range(8):
            loads.append(pltpu.make_async_copy(wh_hbm.at[p], hidden_w.at[p], local_sem.at[p]))
            loads[-1].start()
        start, rest = prepare(
            ends, actions, policy, valid, small, wv, wa, wide, head, keep, info, value_w, adv_w, spread, group
        )
        start = jnp.concatenate([start] * 8, axis=1)
        even[...] = (state_h[...].astype(F32) * start).astype(BF16)
        cell[...] = state_c[...].astype(F32) * start
        act[...] = jnp.broadcast_to(rest(), (8, 512))
        for to in (other, facing, diagonal):
            told.append(copies.push(info.at[head], to))
        loads[0].wait()
        for part in range(3):
            row = iota((256, 768), 0)
            order = ones_where(iota((256, 768), 1) == (row & 31) * 24 + (row >> 5) + 8 * part, BF16)
            got = jnp.dot(order, raw[...], preferred_element_type=F32)
            feat[256 * part : 256 * part + 256, :] = got.astype(BF16)

    gather(me, shard, full, copies, meanwhile)
    for copy in told:
        copy.wait_recv()
    lane = iota((128, 256), 1)
    row = iota((128, 256), 0)
    step_at = (lane >> 5) == (row & 7)
    for s in range(4):
        mine = info[s, 0:1, :] == ((row >> 4) + 8 * head).astype(F32)
        cap = info[s, 8:9, :] == ((row >> 3) & 1).astype(F32)
        pick[s] = ones_where(mine & cap & step_at, BF16)

    def project(rows):
        f = feat[rows, :]
        for hp in range(4):
            for pair in range(2):
                tiles = [
                    full[hp % 2, :, :, hp // 2, :, 2 * pair + g, 0:16, :].reshape(512, 256)
                    for g in range(2)
                ]
                got = jnp.dot(f, jnp.concatenate(tiles, axis=1), preferred_element_type=F32)
                for g in range(2):
                    at = 2 * pair + g
                    line = bias[at : at + 1, hp * 256 : hp * 256 + 256]
                    pre[hp * 4 + at, rows, :] = got[:, g * 256 : g * 256 + 256] + line

    project(slice(0, 12 * seqs))

    def step(t, src, dst, save):
        h = src[...]
        h = jnp.concatenate([h, h, h, h], axis=0)
        alive = keep[t + 1]
        alive = jnp.concatenate([alive, alive], axis=1)
        rows = pl.ds(pl.multiple_of(t * seqs, seqs), seqs)
        for hp in range(4):
            gate = []
            for g in range(4):
                w = full[hp % 2, :, :, hp // 2, :, g, 16:48, :].reshape(1024, 256)
                got = jnp.dot(h, w, preferred_element_type=F32)[0:seqs]
                gate.append(got + pre[hp * 4 + g, rows, :])
            cols = slice(hp * 256, hp * 256 + 256)
            c = sigmoid(gate[1]) * cell[:, cols] + sigmoid(gate[0]) * jnp.tanh(gate[2])
            new = sigmoid(gate[3]) * jnp.tanh(c)
            cell[:, cols] = c * alive
            dst[:, cols] = (new * alive).astype(BF16)
            if save:
                learned[head, t - 8, :, cols] = new.astype(BF16)

    def route(kind, i, owner, to):
        ref = learned.at[head_of(owner), i]
        return pltpu.make_async_remote_copy(
            src_ref=ref,
            dst_ref=ref,
            send_sem=route_send.at[kind, i],
            recv_sem=route_recv.at[kind, i],
            device_id=device(to),
            device_id_type=MESH,
        )

    def send_out(i):
        route(1, i, me, facing).start()
        route(0, i, me, other).start()

    def hand_on(i):
        route(1, i, me, facing).wait_recv()
        route(2, i, facing, other).start()

    def burn(i, _):
        for u in range(4):
            src, dst = (odd, even) if u % 2 else (even, odd)
            step(4 * i + u, src, dst, False)
        return 0

    lag = 6

    def learn(i, _):
        for u in range(4):
            at = 4 * i + u
            if u == 0:

                @pl.when(i > 0)
                def _():
                    send_out(at - 1)

            else:
                send_out(at - 1)

            @pl.when(at >= lag)
            def _():
                hand_on(at - lag)

            src, dst = (odd, even) if u % 2 else (even, odd)
            step(at + 8, src, dst, True)

        @pl.when(i < 3)
        def _():
            project(pl.ds(pl.multiple_of((4 * i + 12) * seqs, 128), 128))

        return 0

    lax.fori_loop(0, 2, burn, 0)
    lax.fori_loop(0, 4, learn, 0)
    send_out(15)

    def pack(s, half):
        rows = learned[s, 8 * half : 8 * half + 8].reshape(256, 1024)
        got = jnp.dot(pick[s], rows, preferred_element_type=F32).astype(BF16)
        packed[:, (2 * s + half) * 16 : (2 * s + half) * 16 + 16, :] = got.reshape(8, 16, 1024)

    for load in loads[1:]:
        load.wait()
    for i in range(16 - lag, 16):
        hand_on(i)
    for i in range(8):
        route(0, i, me, other).wait_recv()
        route(2, i, facing, other).wait_recv()
    for s in range(4):
        pack(s, 0)
    for i in range(8, 16):
        route(0, i, me, other).wait_recv()
        route(2, i, facing, other).wait_recv()
    for s in range(4):
        pack(s, 1)
    valid_lane = iota((128, 128), 1) < ACTIONS
    for quad in range(2):
        total = None
        for j in range(4):
            p = 4 * quad + j
            mid = jnp.dot(packed[p], hidden_w[p], preferred_element_type=F32)
            mid = jnp.maximum(mid, 0.0).astype(BF16)
            value = jnp.dot(mid[:, 0:512], value_w[p], preferred_element_type=F32)
            adv = jnp.dot(mid[:, 512:1024], adv_w[p], preferred_element_type=F32)
            q = value + adv - jnp.sum(adv, axis=1, keepdims=True) * (1.0 / ACTIONS)
            q = jnp.where(valid_lane, q, 0.0)
            if j:
                q = pltpu.roll(q, 32 * j, 1)
            total = q if total is None else total + q
        for s in range(4):
            answers[s, 32 * quad : 32 * quad + 32, :] = total[32 * s : 32 * s + 32].astype(BF16)
    replies[head] = answers[head]
    back = []
    for to in (diagonal, facing, other):
        back.append(copies.send(answers.at[head_of(to)], replies.at[head], to))
    for copy in back:
        copy.wait_recv()
    got = replies[...].reshape(256, 128).astype(F32).T.astype(BF16)
    found = jnp.dot(got, spread[...], preferred_element_type=F32) * group[...]
    found = found[0:32] + found[32:64] + found[64:96] + found[96:128]
    chosen = jnp.where(iota((32, 512), 0).astype(F32) == act[0:1, :], found, 0.0)
    taken = jnp.sum(chosen, axis=0, keepdims=True)
    for t in range(16):
        tile, off = t // 4 * 128, t % 4 * 32
        now = found[0:24, tile : tile + 128]
        mine = jnp.broadcast_to(taken[:, tile : tile + 128], (8, 128))
        if off:
            now = pltpu.roll(now, 128 - off, 1)
            mine = pltpu.roll(mine, 128 - off, 1)
        q_out[pl.ds(t, ACTIONS, stride=16), :] = now[0:ACTIONS, 0:32]
        taken_out[t : t + 1, :] = mine[0:1, 0:32]
    for i in range(16):
        route(0, i, me, other).wait_send()
        route(1, i, me, facing).wait_send()
        route(2, i, facing, other).wait_send()
    for copy in copies.sent:
        copy.wait_send()


def shards(
    features,
    state_h,
    state_c,
    valid,
    ends,
    policy,
    actions,
    w_input,
    w_recur,
    lstm_bias,
    w_hidden,
    w_value,
    w_advantage,
):
    vmem = pl.BlockSpec(memory_space=pltpu.VMEM)
    hbm = pl.BlockSpec(memory_space=pl.ANY)
    dma = pltpu.SemaphoreType.DMA
    q, taken = pl.pallas_call(
        core_kernel,
        out_shape=(
            jax.ShapeDtypeStruct((ACTIONS * 16, 32), F32),
            jax.ShapeDtypeStruct((16, 32), F32),
        ),
        in_specs=[vmem] * 11 + [hbm] * 2,
        out_specs=(vmem, vmem),
        scratch_shapes=[
            pltpu.VMEM((4, 48, 256), BF16),
            pltpu.VMEM((2, 4, 2, 2, 4, 4, 48, 256), BF16),
            pltpu.VMEM((16, 768, 256), F32),
            pltpu.VMEM((32, 1024), BF16),
            pltpu.VMEM((32, 1024), BF16),
            pltpu.VMEM((32, 1024), F32),
            pltpu.VMEM((25, 32, 128), F32),
            pltpu.VMEM((768, 512), BF16),
            pltpu.VMEM((768, 512), BF16),
            pltpu.VMEM((8, 1024, 1024), BF16),
            pltpu.VMEM((4, 16, 32, 1024), BF16),
            pltpu.VMEM((8, 128, 1024), BF16),
            pltpu.VMEM((128, 128), F32),
            pltpu.VMEM((1024, 128), F32),
            pltpu.VMEM((4, 16, 256), F32),
            pltpu.VMEM((4, 128, 256), BF16),
            pltpu.VMEM((8, 512, 128), BF16),
            pltpu.VMEM((8, 512, 128), BF16),
            pltpu.VMEM((256, 512), BF16),
            pltpu.VMEM((128, 512), F32),
            pltpu.VMEM((8, 512), F32),
            pltpu.VMEM((4, 64, 128), BF16),
            pltpu.VMEM((4, 64, 128), BF16),
            dma((9,)),
            dma((SENDS,)),
            dma((SENDS,)),
            dma((3, 16)),
            dma((3, 16)),
        ],
        compiler_params=pltpu.CompilerParams(
            collective_id=0, has_side_effects=True, vmem_limit_bytes=60 * 2**20
        ),
        name="core",
    )(
        w_input,
        w_recur,
        ends.T,
        actions.T,
        policy.T,
        valid[None, :],
        lstm_bias,
        w_value,
        w_advantage.transpose(2, 0, 1),
        state_h,
        state_c,
        features.reshape(-1, features.shape[2]),
        w_hidden,
    )
    return q.reshape(ACTIONS, 16, 32).transpose(2, 1, 0), taken.T


def solution(mesh):
    return jax.shard_map(
        shards,
        mesh=mesh,
        in_specs=(
            P(("batch", "head"), None, None),
            P(("batch", "head"), None),
            P(("batch", "head"), None),
            P(("batch", "head")),
            P(("batch", "head"), None),
            P(("batch", "head"), None),
            P(("batch", "head"), None),
            P("batch", None, "head"),
            P("batch", None, "head"),
            P(),
            P("head", None, None),
            P("head", None),
            P("head", None, None),
        ),
        out_specs=(P(("batch", "head"), None, None), P(("batch", "head"), None)),
        check_vma=False,
    )
```

time: 112 us -> 91.8 us (0.82)
  local copies, waits for them, and re-layouts: 12.4 us -> 2.88 us
  Pallas kernels: 96.6 us -> 88.1 us
  other arithmetic: 1.34 us -> 0 us
    pallas_call x1, Pallas kernels: 96.6 us -> 88.1 us  [shards(): pl.pallas_call(core_kernel, out_shape=(jax.ShapeDtypeStruct((ACTIONS * 16...]
    unnamed x6 -> x2, local copies, waits for them, and re-layouts: 6.22 us -> 2.88 us
    pallas_call x2 -> x0, local copies, waits for them, and re-layouts: 3.18 us -> none  [shards(): pl.pallas_call(core_kernel, out_shape=(jax.ShapeDtypeStruct((32, 16, ACTI...]
    transpose x1 -> x0, local copies, waits for them, and re-layouts: 2.29 us -> none  [shards(): feat = features.transpose(1, 0, 2).reshape(-1, features.shape[2])]
where the time goes in v3:
time: 91.8 us; the launch traced here: 91.6 us
  Pallas kernels  88.1 us (96%)
  local copies, waits for them, and re-layouts  2.88 us (3%)
    pallas_call x1, Pallas kernels, shards(): pl.pallas_call(core_kernel, out_shape=(jax.ShapeDtypeStruct((ACTIONS * 16...  88.1 us
    unnamed x2, local copies, waits for them, and re-layouts  2.88 us

profile of v3, /device:TPU:1, one launch (start us, length us, event | category | flops | bytes accessed | tf_op | source)
XLA Modules:
  0.0 91.6 jit_solution(6067638564310053319)
XLA Ops:
  0.6 88.1 %core.1 = (f32[288,32]{1,0:T(8,128)}, f32[16,32]{1,0:T(8,128)}) custom-call(bf16[16,4,256]{2,1,0:T(4,128)(2,1)} %w_in.1, bf16[32,4,256]{2,1,0:T(4,128)(2,1)} %w_rec.1, s32[24,32]{1,0:T(8,128)} %bitcast.13, s32[16,32]{1,0:T(8,128)} %bitcast.14, s32[1,32]{1,0:T(1,128)} %bitcast.16, s32[1,32]{1,0:T(1,128)} %bitcast.17, f32[4,1024]{1,0:T(4,128)} %bias.1, ...), custom_call_target="tpu_custom_call" | custom-call | tf_op jit(solution)/shard_map/core/pallas_call | solution.py:471
  88.8 1.6 %copy.17 = f32[32,16,18]{0,1,2:T(8,128)} copy(f32[32,16,18]{0,1,2:T(8,128)} %bitcast.11) | data formatting | bytes 73728
  90.3 1.3 %copy.18 = f32[32,16]{0,1:T(8,128)} copy(f32[32,16]{0,1:T(8,128)} %bitcast.15) | data formatting | bytes 4096

commit v4 on v3

--- a/solution.py
+++ b/solution.py
@@ -27,14 +27,14 @@
     return {**at, axis: (at[axis] + by + 4) % 4}
 
 
-def entry_barrier(me):
+def greet(me):
     barrier = pltpu.get_barrier_semaphore()
     other = {**me, "c": 1 - me["c"]}
     peers = [shifted(me, a, d) for a in "xyz" for d in (1, -1, 2)]
     peers += [other, {**other, "y": me["y"] + 1 - 2 * (me["y"] % 2)}]
     for p in peers:
         pl.semaphore_signal(barrier, inc=1, device_id=device(p), device_id_type=MESH)
-    pl.semaphore_wait(barrier, len(peers))
+    return lambda: pl.semaphore_wait(barrier, len(peers))
 
 
 class Copies:
@@ -60,7 +60,7 @@
         return self.send(ref, ref, to)
 
 
-def gather(me, shard, full, copies, meanwhile):
+def gather(me, shard, full, copies, meanwhile, later):
     other = {**me, "c": 1 - me["c"]}
     crossed = []
 
@@ -124,6 +124,7 @@
         at = shifted(me, b, 2)
         along_last(k, 3, at)
         cross(region(k, at, free=a))
+    later()
     relay = {}
     offsets = (0, -1, 1, 2)
     for m in range(4):
@@ -165,9 +166,12 @@
     for t in range(24):
         keep[t] = jnp.broadcast_to(1.0 - by_seq[0:32, t : t + 1], (32, 128))
     keep[24] = jnp.ones((32, 128), F32)
-    rows = small[24:48, :]
-    rows = rows + pltpu.roll(rows, 32, 1) + pltpu.roll(rows, 64, 1) + pltpu.roll(rows, 96, 1)
-    across = rows[16:17, :]
+
+    def tiled():
+        rows = small[24:48, :]
+        return rows + pltpu.roll(rows, 32, 1) + pltpu.roll(rows, 64, 1) + pltpu.roll(rows, 96, 1)
+
+    across = tiled()[16:17, :]
     same = jnp.broadcast_to(by_seq[0:32, 40:41], (32, 128)) == across
     earlier = iota((32, 128), 0) < (iota((32, 128), 1) & 31)
     rank = jnp.sum(ones_where(same & earlier, F32), axis=0, keepdims=True)
@@ -177,6 +181,7 @@
     start = jnp.broadcast_to(by_seq[0:32, 41:42], (32, 128)) * keep[0]
 
     def finish():
+        rows, across, rank = tiled(), info[head, 0:1, 0:128], info[head, 8:9, 0:128]
         lane = iota((1, 512), 1)
         step = lane >> 5
         number = jnp.concatenate([across] * 4, axis=1).astype(jnp.int32)
@@ -203,88 +208,100 @@
     return start, finish
 
 
-def core_kernel(
-    w_in,
-    w_rec,
-    ends,
-    actions,
-    policy,
-    valid,
-    bias,
-    wv,
-    wa,
-    state_h,
-    state_c,
-    feat_hbm,
-    wh_hbm,
-    q_out,
-    taken_out,
-    shard,
-    full,
-    pre,
-    even,
-    odd,
-    cell,
-    keep,
-    raw,
-    feat,
-    hidden_w,
-    learned,
-    packed,
-    small,
-    wide,
-    info,
-    pick,
-    value_w,
-    adv_w,
-    spread,
-    group,
-    act,
-    answers,
-    replies,
-    local_sem,
-    send_sem,
-    recv_sem,
-    route_send,
-    route_recv,
-):
+class Unit:
+    def __init__(self, number, accs):
+        self.number = number
+        self.gates, self.spare, self.wide = accs
+        self.turn = 0
+
+    def push(self, tile, slot):
+        pltpu.matmul_push_rhs(tile, staging_register=slot, mxu_index=self.number)
+
+    def run(self, acc, pairs):
+        for rows, tile in pairs:
+            self.push(tile, self.turn)
+            pltpu.matmul_acc_lhs(acc, rows, load_staged_rhs=self.turn)
+            self.turn = 1 - self.turn
+        return acc
+
+
+def accumulators(number):
+    acc = pltpu.ACC(number)
+    return (
+        [acc((32, 256), F32) for _ in range(8)],
+        acc((96, 256), F32),
+        [acc((128, 256), F32) for _ in range(5)],
+    )
+
+
+def core_kernel(*refs):
+    pl.run_scoped(lambda first, second: core(refs, (Unit(0, first), Unit(1, second))), accumulators(0), accumulators(1))
+
+
+def core(refs, units):
+    given, (q_out, taken_out), held = refs[:13], refs[13:15], refs[15:26]
+    w_in, w_rec, ends, actions, policy, valid, bias, wv, wa, state_h, state_c = held
+    (
+        shard, full, pre, even, odd, cell, keep, feat, hidden_w, learned, packed, small, wide, info, pick,
+        value_w, adv_w, spread, group, act, answers, replies, local_sem, send_sem, recv_sem, route_send, route_recv,
+    ) = refs[26:]
+    wh_hbm = given[12]
     me = here()
+    met = greet(me)
+    for unit in units:
+        for acc in unit.gates + [unit.spare] + unit.wide:
+            pltpu.matmul_pop(acc)
     seqs = 32
     head = me["y"] % 2 * 2 + me["c"]
     other = {**me, "c": 1 - me["c"]}
     facing = {**me, "y": me["y"] + 1 - 2 * (me["y"] % 2)}
     diagonal = {**facing, "c": 1 - me["c"]}
     head_of = lambda at: at["y"] % 2 * 2 + at["c"]
-    loads = [pltpu.make_async_copy(feat_hbm, raw, local_sem.at[8])]
-    loads[0].start()
+    raw = packed.at[0:6, :, 0:512]
+    loads = [pltpu.make_async_copy(given[k], ref, local_sem.at[8 + k]) for k, ref in enumerate(held + (raw,))]
+    for load in loads:
+        load.start()
+    for load in loads[0:2]:
+        load.wait()
     for g in range(4):
         shard[g, 0:16, :] = w_in[:, g, :]
         shard[g, 16:48, :] = w_rec[:, g, :]
-    entry_barrier(me)
+    met()
     copies = Copies(send_sem, recv_sem)
     told = []
+    rest = []
+    weights = [pltpu.make_async_copy(wh_hbm.at[p], hidden_w.at[p], local_sem.at[p]) for p in range(8)]
 
     def meanwhile():
-        for p in range(8):
-            loads.append(pltpu.make_async_copy(wh_hbm.at[p], hidden_w.at[p], local_sem.at[p]))
-            loads[-1].start()
-        start, rest = prepare(
+        for load in loads[2:]:
+            load.wait()
+        start, finish = prepare(
             ends, actions, policy, valid, small, wv, wa, wide, head, keep, info, value_w, adv_w, spread, group
         )
+        rest.append(finish)
         start = jnp.concatenate([start] * 8, axis=1)
         even[...] = (state_h[...].astype(F32) * start).astype(BF16)
         cell[...] = state_c[...].astype(F32) * start
-        act[...] = jnp.broadcast_to(rest(), (8, 512))
         for to in (other, facing, diagonal):
             told.append(copies.push(info.at[head], to))
-        loads[0].wait()
-        for part in range(3):
-            row = iota((256, 768), 0)
-            order = ones_where(iota((256, 768), 1) == (row & 31) * 24 + (row >> 5) + 8 * part, BF16)
-            got = jnp.dot(order, raw[...], preferred_element_type=F32)
-            feat[256 * part : 256 * part + 256, :] = got.astype(BF16)
-
-    gather(me, shard, full, copies, meanwhile)
+        for load in weights:
+            load.start()
+
+    def later():
+        act[...] = jnp.broadcast_to(rest[0](), (8, 512))
+        for part in range(6):
+            row = iota((128, 768), 0)
+            order = ones_where(iota((128, 768), 1) == (row & 31) * 24 + (row >> 5) + 4 * part, BF16)
+            for n, unit in enumerate(units):
+                cols = slice(256 * n, 256 * n + 256)
+                pairs = [
+                    (order[:, 256 * k : 256 * k + 256], packed[2 * k : 2 * k + 2, :, cols].reshape(256, 256))
+                    for k in range(3)
+                ]
+                got = pltpu.matmul_pop(unit.run(unit.wide[part % 4], pairs))
+                feat[128 * part : 128 * part + 128, cols] = got.astype(BF16)
+
+    gather(me, shard, full, copies, meanwhile, later)
     for copy in told:
         copy.wait_recv()
     lane = iota((128, 256), 1)
@@ -295,44 +312,72 @@
         cap = info[s, 8:9, :] == ((row >> 3) & 1).astype(F32)
         pick[s] = ones_where(mine & cap & step_at, BF16)
 
-    def project(rows):
-        f = feat[rows, :]
-        for hp in range(4):
-            for pair in range(2):
-                tiles = [
-                    full[hp % 2, :, :, hp // 2, :, 2 * pair + g, 0:16, :].reshape(512, 256)
-                    for g in range(2)
-                ]
-                got = jnp.dot(f, jnp.concatenate(tiles, axis=1), preferred_element_type=F32)
-                for g in range(2):
-                    at = 2 * pair + g
-                    line = bias[at : at + 1, hp * 256 : hp * 256 + 256]
-                    pre[hp * 4 + at, rows, :] = got[:, g * 256 : g * 256 + 256] + line
-
-    project(slice(0, 12 * seqs))
-
-    def step(t, src, dst, save):
-        h = src[...]
-        h = jnp.concatenate([h, h, h, h], axis=0)
+    def project(start):
+        rows = pl.ds(start, 128)
+        f = [feat[rows, 256 * k : 256 * k + 256] for k in range(2)]
+        for n in range(16):
+            hp, g = n // 4, n % 4
+            unit = units[n % 2]
+            pairs = [
+                (f[k], full[hp % 2, 2 * k : 2 * k + 2, :, hp // 2, :, g, 0:16, :].reshape(256, 256))
+                for k in range(2)
+            ]
+            got = pltpu.matmul_pop(unit.run(unit.wide[n // 2 % 4], pairs))
+            pre[n, rows, :] = got + bias[g : g + 1, hp * 256 : hp * 256 + 256]
+
+    for part in range(3):
+        project(128 * part)
+
+    tiles = [(hp, pair, 0) for hp in range(4) for pair in range(2)]
+    tiles += [(hp, pair, k) for hp in range(4) for k in range(1, 4) for pair in range(2)]
+
+    def stage(i):
+        hp, pair, k = tiles[i % 32]
+        for q, unit in enumerate(units):
+            w = full[hp % 2, k, :, hp // 2, :, 2 * pair + q, 16:48, :].reshape(256, 256)
+            unit.push(w, i % 2)
+
+    def multiply(src, first, last, ahead=True):
+        for i in range(first, last):
+            if ahead or i + 1 < last:
+                stage(i + 1)
+            hp, pair, k = tiles[i]
+            h = src[:, 256 * k : 256 * k + 256]
+            for unit in units:
+                pltpu.matmul_acc_lhs(unit.gates[2 * hp + pair], h, load_staged_rhs=i % 2)
+            h = jnp.concatenate([h, h, h], axis=0)
+            for unit in units:
+                pltpu.matmul_acc_lhs(unit.spare, h)
+
+    def settle(t, hp, dst, save):
+        rows = pl.ds(pl.multiple_of(t * seqs, seqs), seqs)
         alive = keep[t + 1]
         alive = jnp.concatenate([alive, alive], axis=1)
-        rows = pl.ds(pl.multiple_of(t * seqs, seqs), seqs)
-        for hp in range(4):
-            gate = []
-            for g in range(4):
-                w = full[hp % 2, :, :, hp // 2, :, g, 16:48, :].reshape(1024, 256)
-                got = jnp.dot(h, w, preferred_element_type=F32)[0:seqs]
-                gate.append(got + pre[hp * 4 + g, rows, :])
-            cols = slice(hp * 256, hp * 256 + 256)
-            c = sigmoid(gate[1]) * cell[:, cols] + sigmoid(gate[0]) * jnp.tanh(gate[2])
-            new = sigmoid(gate[3]) * jnp.tanh(c)
-            cell[:, cols] = c * alive
-            dst[:, cols] = (new * alive).astype(BF16)
-            if save:
-                learned[head, t - 8, :, cols] = new.astype(BF16)
+        gate = [pltpu.matmul_pop(units[g % 2].gates[2 * hp + g // 2]) for g in range(4)]
+        gate = [gate[g] + pre[hp * 4 + g, rows, :] for g in range(4)]
+        cols = slice(hp * 256, hp * 256 + 256)
+        c = sigmoid(gate[1]) * cell[:, cols] + sigmoid(gate[0]) * jnp.tanh(gate[2])
+        new = sigmoid(gate[3]) * jnp.tanh(c)
+        cell[:, cols] = c * alive
+        dst[:, cols] = (new * alive).astype(BF16)
+        if save:
+            learned[head, t - 7, :, cols] = new.astype(BF16)
+
+    def step(t, src, dst, save, begin=False, ahead=True, between=None):
+        multiply(src, 0, 6)
+        if not begin:
+            settle(t - 1, 3, src, save)
+        multiply(src, 6, 20)
+        if between is not None:
+            between()
+        settle(t, 0, dst, save)
+        multiply(src, 20, 26)
+        settle(t, 1, dst, save)
+        multiply(src, 26, 32, ahead)
+        settle(t, 2, dst, save)
 
     def route(kind, i, owner, to):
-        ref = learned.at[head_of(owner), i]
+        ref = learned.at[head_of(owner), i + 1]
         return pltpu.make_async_remote_copy(
             src_ref=ref,
             dst_ref=ref,
@@ -351,48 +396,59 @@
         route(2, i, facing, other).start()
 
     def burn(i, _):
-        for u in range(4):
-            src, dst = (odd, even) if u % 2 else (even, odd)
-            step(4 * i + u, src, dst, False)
+        step(2 * i, even, odd, False)
+        step(2 * i + 1, odd, even, False)
         return 0
 
     lag = 6
 
     def learn(i, _):
+        stage(0)
         for u in range(4):
             at = 4 * i + u
-            if u == 0:
-
-                @pl.when(i > 0)
+
+            def exchange():
+                if u:
+                    send_out(at - 1)
+                else:
+
+                    @pl.when(i > 0)
+                    def _():
+                        send_out(at - 1)
+
+                @pl.when(at >= lag)
                 def _():
-                    send_out(at - 1)
-
-            else:
-                send_out(at - 1)
-
-            @pl.when(at >= lag)
-            def _():
-                hand_on(at - lag)
+                    hand_on(at - lag)
 
             src, dst = (odd, even) if u % 2 else (even, odd)
-            step(at + 8, src, dst, True)
+            step(at + 8, src, dst, True, ahead=u < 3, between=exchange)
 
         @pl.when(i < 3)
         def _():
-            project(pl.ds(pl.multiple_of((4 * i + 12) * seqs, 128), 128))
+            project(pl.multiple_of((4 * i + 12) * seqs, 128))
 
         return 0
 
-    lax.fori_loop(0, 2, burn, 0)
+    stage(0)
+    step(0, even, odd, False, begin=True)
+    step(1, odd, even, False)
+    lax.fori_loop(1, 3, burn, 0)
+    step(6, even, odd, False)
+    step(7, odd, even, False, ahead=False)
     lax.fori_loop(0, 4, learn, 0)
+    settle(23, 3, even, True)
     send_out(15)
+    for unit in units:
+        pltpu.matmul_pop(unit.spare)
 
     def pack(s, half):
-        rows = learned[s, 8 * half : 8 * half + 8].reshape(256, 1024)
-        got = jnp.dot(pick[s], rows, preferred_element_type=F32).astype(BF16)
-        packed[:, (2 * s + half) * 16 : (2 * s + half) * 16 + 16, :] = got.reshape(8, 16, 1024)
-
-    for load in loads[1:]:
+        for n in range(4):
+            unit, cols = units[n % 2], slice(256 * n, 256 * n + 256)
+            rows = learned[s, 8 * half + 1 : 8 * half + 9, :, cols].reshape(256, 256)
+            got = pltpu.matmul_pop(unit.run(unit.wide[2 * (s % 2) + n // 2], [(pick[s], rows)]))
+            packed[:, (2 * s + half) * 16 : (2 * s + half) * 16 + 16, cols] = got.astype(BF16).reshape(8, 16, 256)
+
+    for load in weights:
         load.wait()
     for i in range(16 - lag, 16):
         hand_on(i)
@@ -407,16 +463,40 @@
     for s in range(4):
         pack(s, 1)
     valid_lane = iota((128, 128), 1) < ACTIONS
+    def inner(p):
+        accs = []
+        for n in range(4):
+            unit, cols = units[n % 2], slice(256 * n, 256 * n + 256)
+            pairs = [
+                (packed[p, :, 256 * k : 256 * k + 256], hidden_w[p, 256 * k : 256 * k + 256, cols])
+                for k in range(4)
+            ]
+            accs.append(unit.run(unit.wide[2 * (p % 2) + n // 2], pairs))
+        return accs
+
+    def outer(p, accs):
+        mid = [jnp.maximum(pltpu.matmul_pop(acc), 0.0).astype(BF16) for acc in accs]
+        nil = jnp.zeros((256, 128), BF16)
+        pairs = []
+        for k in range(4):
+            part = slice(256 * (k % 2), 256 * (k % 2) + 256)
+            if k < 2:
+                tile = [value_w[p, part, :], nil]
+            else:
+                tile = [adv_w[p, part, :]] * 2
+            pairs.append((mid[k], jnp.concatenate(tile, axis=1)))
+        unit = units[p % 2]
+        got = pltpu.matmul_pop(unit.run(unit.wide[4], pairs))
+        mean = jnp.sum(got[:, 128:256], axis=1, keepdims=True) * (1.0 / ACTIONS)
+        return jnp.where(valid_lane, got[:, 0:128] - mean, 0.0)
+
+    ready = inner(0)
     for quad in range(2):
         total = None
         for j in range(4):
             p = 4 * quad + j
-            mid = jnp.dot(packed[p], hidden_w[p], preferred_element_type=F32)
-            mid = jnp.maximum(mid, 0.0).astype(BF16)
-            value = jnp.dot(mid[:, 0:512], value_w[p], preferred_element_type=F32)
-            adv = jnp.dot(mid[:, 512:1024], adv_w[p], preferred_element_type=F32)
-            q = value + adv - jnp.sum(adv, axis=1, keepdims=True) * (1.0 / ACTIONS)
-            q = jnp.where(valid_lane, q, 0.0)
+            now, ready = ready, inner(p + 1) if p < 7 else None
+            q = outer(p, now)
             if j:
                 q = pltpu.roll(q, 32 * j, 1)
             total = q if total is None else total + q
@@ -429,7 +509,11 @@
     for copy in back:
         copy.wait_recv()
     got = replies[...].reshape(256, 128).astype(F32).T.astype(BF16)
-    found = jnp.dot(got, spread[...], preferred_element_type=F32) * group[...]
+    found = [
+        pltpu.matmul_pop(unit.run(unit.wide[0], [(got, spread[:, 256 * n : 256 * n + 256])]))
+        for n, unit in enumerate(units)
+    ]
+    found = jnp.concatenate(found, axis=1) * group[...]
     found = found[0:32] + found[32:64] + found[64:96] + found[96:128]
     chosen = jnp.where(iota((32, 512), 0).astype(F32) == act[0:1, :], found, 0.0)
     taken = jnp.sum(chosen, axis=0, keepdims=True)
@@ -466,17 +550,36 @@
     w_advantage,
 ):
     vmem = pl.BlockSpec(memory_space=pltpu.VMEM)
-    hbm = pl.BlockSpec(memory_space=pl.ANY)
+    held = [(16, 4, 256), (32, 4, 256), (24, 32), (16, 32), (1, 32), (1, 32), (4, 1024), (8, 512), (ACTIONS, 8, 512)]
+    held += [(32, 1024), (32, 1024)]
+    kinds = [BF16] * 2 + [jnp.int32] * 4 + [F32] + [BF16] * 4
     dma = pltpu.SemaphoreType.DMA
+    given = (
+        w_input,
+        w_recur,
+        ends.T,
+        actions.T,
+        policy.T,
+        valid[None, :],
+        lstm_bias,
+        w_value,
+        w_advantage.transpose(2, 0, 1),
+        state_h,
+        state_c,
+        features.reshape(6, 128, features.shape[2]),
+        w_hidden,
+    )
+    pinned = [pltpu.with_memory_space_constraint(v, pltpu.HBM) for v in given]
     q, taken = pl.pallas_call(
         core_kernel,
         out_shape=(
             jax.ShapeDtypeStruct((ACTIONS * 16, 32), F32),
             jax.ShapeDtypeStruct((16, 32), F32),
         ),
-        in_specs=[vmem] * 11 + [hbm] * 2,
+        in_specs=[pl.BlockSpec(memory_space=pltpu.HBM)] * 13,
         out_specs=(vmem, vmem),
-        scratch_shapes=[
+        scratch_shapes=[pltpu.VMEM(shape, kind) for shape, kind in zip(held, kinds)]
+        + [
             pltpu.VMEM((4, 48, 256), BF16),
             pltpu.VMEM((2, 4, 2, 2, 4, 4, 48, 256), BF16),
             pltpu.VMEM((16, 768, 256), F32),
@@ -485,9 +588,8 @@
             pltpu.VMEM((32, 1024), F32),
             pltpu.VMEM((25, 32, 128), F32),
             pltpu.VMEM((768, 512), BF16),
-            pltpu.VMEM((768, 512), BF16),
             pltpu.VMEM((8, 1024, 1024), BF16),
-            pltpu.VMEM((4, 16, 32, 1024), BF16),
+            pltpu.VMEM((4, 17, 32, 1024), BF16),
             pltpu.VMEM((8, 128, 1024), BF16),
             pltpu.VMEM((128, 128), F32),
             pltpu.VMEM((1024, 128), F32),
@@ -500,31 +602,17 @@
             pltpu.VMEM((8, 512), F32),
             pltpu.VMEM((4, 64, 128), BF16),
             pltpu.VMEM((4, 64, 128), BF16),
-            dma((9,)),
+            dma((20,)),
             dma((SENDS,)),
             dma((SENDS,)),
             dma((3, 16)),
             dma((3, 16)),
         ],
         compiler_params=pltpu.CompilerParams(
-            collective_id=0, has_side_effects=True, vmem_limit_bytes=60 * 2**20
+            collective_id=0, has_side_effects=True, vmem_limit_bytes=int(53.5 * 2**20)
         ),
         name="core",
-    )(
-        w_input,
-        w_recur,
-        ends.T,
-        actions.T,
-        policy.T,
-        valid[None, :],
-        lstm_bias,
-        w_value,
-        w_advantage.transpose(2, 0, 1),
-        state_h,
-        state_c,
-        features.reshape(-1, features.shape[2]),
-        w_hidden,
-    )
+    )(*pinned)
     return q.reshape(ACTIONS, 16, 32).transpose(2, 1, 0), taken.T
 
 

time: 91.8 us -> 87 us (0.948)
  Pallas kernels: 88.1 us -> 85 us
  local copies, waits for them, and re-layouts: 2.88 us -> 1.26 us
    pallas_call x1, Pallas kernels: 88.1 us -> 85 us  [shards(): pl.pallas_call(core_kernel, out_shape=(jax.ShapeDtypeStruct((ACTIONS * 16...]
    unnamed x2, local copies, waits for them, and re-layouts: 2.88 us -> 1.26 us
where the time goes in v4:
time: 87 us; the launch traced here: 86.9 us
  Pallas kernels  85 us (98%)
  local copies, waits for them, and re-layouts  1.26 us (1%)
    pallas_call x1, Pallas kernels, shards(): pl.pallas_call(core_kernel, out_shape=(jax.ShapeDtypeStruct((ACTIONS * 16...  85 us

profile of v4, /device:TPU:1, one launch (start us, length us, event | category | flops | bytes accessed | tf_op | source)
XLA Modules:
  0.0 86.9 jit_solution(7551615289519035275)
XLA Ops:
  0.6 85.0 %core.1 = (f32[288,32]{1,0:T(8,128)S(1)}, f32[16,32]{1,0:T(8,128)S(1)}) custom-call(bf16[16,4,256]{2,1,0:T(4,128)(2,1)} %refs_0_.1, bf16[32,4,256]{2,1,0:T(4,128)(2,1)} %refs_1_.1, s32[24,32]{1,0:T(8,128)} %bitcast.14, s32[16,32]{1,0:T(8,128)} %bitcast.15, s32[1,32]{1,0:T(1,128)} %bitcast.16, s32[1,32]{1,0:T(1,128)} %bitcast.17, f32[4,1024]{1,0:T(4,128)} %refs_6_.1, ...), custom_call_target="tpu_custom_call" | custom-call | tf_op jit(solution)/shard_map/core/pallas_call | solution.py:573
  85.7 0.7 copy.17
  86.3 0.6 copy.18

commit v5 on v4

--- a/solution.py
+++ b/solution.py
@@ -62,7 +62,7 @@
 
 def gather(me, shard, full, copies, meanwhile, later):
     other = {**me, "c": 1 - me["c"]}
-    crossed = []
+    crossed = {k: [] for k in range(3)}
 
     def region(part, at, free=None, half=None):
         z, x = at["z"], at["x"]
@@ -74,8 +74,8 @@
             z, x = (span, x) if free == "z" else (z, span)
         return full.at[me["c"], z, y[0], y[1], x, :, pl.ds(16 * part, 16), :]
 
-    def cross(ref):
-        crossed.append(copies.push(ref, other))
+    def cross(k, ref):
+        crossed[k].append(copies.push(ref, other))
 
     def own(k):
         return shard.at[:, pl.ds(16 * k, 16), :]
@@ -109,7 +109,7 @@
             at = shifted(me, a, -d)
             along_both(k, at, region(k, at))
     for k, (a, b, c) in enumerate(ORDERS):
-        cross(region(k, me, free=a))
+        cross(k, region(k, me, free=a))
     for k, (a, b, c) in enumerate(ORDERS):
         for m, d in ((1, 1), (2, -1)):
             for copy in line[k, d]:
@@ -117,13 +117,13 @@
             at = shifted(me, b, -d)
             relay[k, d] = copies.push(region(k, at, free=a, half=(1 - d) // 2), shifted(me, b, d))
             along_last(k, m, at)
-            cross(region(k, at, free=a))
+            cross(k, region(k, at, free=a))
     for k, (a, b, c) in enumerate(ORDERS):
         for d in (1, -1):
             relay[k, d].wait_recv()
         at = shifted(me, b, 2)
         along_last(k, 3, at)
-        cross(region(k, at, free=a))
+        cross(k, region(k, at, free=a))
     later()
     relay = {}
     offsets = (0, -1, 1, 2)
@@ -134,14 +134,18 @@
                     copy.wait_recv()
                 at = shifted(shifted(me, b, offsets[m]), c, -d)
                 relay[k, m, d] = copies.push(region(k, at, free=a, half=(1 - d) // 2), shifted(me, c, d))
-                cross(region(k, at, free=a))
+                cross(k, region(k, at, free=a))
     for m in range(4):
         for k, (a, b, c) in enumerate(ORDERS):
             for d in (1, -1):
                 relay[k, m, d].wait_recv()
-            cross(region(k, shifted(shifted(me, b, offsets[m]), c, 2), free=a))
-    for copy in crossed:
-        copy.wait_recv()
+            cross(k, region(k, shifted(shifted(me, b, offsets[m]), c, 2), free=a))
+
+    def crossing(k):
+        for copy in crossed[k]:
+            copy.wait_recv()
+
+    return crossing
 
 
 def sigmoid(v):
@@ -301,7 +305,7 @@
                 got = pltpu.matmul_pop(unit.run(unit.wide[part % 4], pairs))
                 feat[128 * part : 128 * part + 128, cols] = got.astype(BF16)
 
-    gather(me, shard, full, copies, meanwhile, later)
+    crossing = gather(me, shard, full, copies, meanwhile, later)
     for copy in told:
         copy.wait_recv()
     lane = iota((128, 256), 1)
@@ -325,8 +329,11 @@
             got = pltpu.matmul_pop(unit.run(unit.wide[n // 2 % 4], pairs))
             pre[n, rows, :] = got + bias[g : g + 1, hp * 256 : hp * 256 + 256]
 
+    crossing(0)
     for part in range(3):
         project(128 * part)
+    crossing(1)
+    crossing(2)
 
     tiles = [(hp, pair, 0) for hp in range(4) for pair in range(2)]
     tiles += [(hp, pair, k) for hp in range(4) for k in range(1, 4) for pair in range(2)]
@@ -367,9 +374,10 @@
         multiply(src, 0, 6)
         if not begin:
             settle(t - 1, 3, src, save)
-        multiply(src, 6, 20)
+        multiply(src, 6, 12)
         if between is not None:
             between()
+        multiply(src, 12, 20)
         settle(t, 0, dst, save)
         multiply(src, 20, 26)
         settle(t, 1, dst, save)
@@ -441,27 +449,30 @@
     for unit in units:
         pltpu.matmul_pop(unit.spare)
 
-    def pack(s, half):
+    def pack(turn, s, half):
+        at = pl.ds(pl.multiple_of((2 * s + half) * 16, 16), 16)
         for n in range(4):
             unit, cols = units[n % 2], slice(256 * n, 256 * n + 256)
             rows = learned[s, 8 * half + 1 : 8 * half + 9, :, cols].reshape(256, 256)
-            got = pltpu.matmul_pop(unit.run(unit.wide[2 * (s % 2) + n // 2], [(pick[s], rows)]))
-            packed[:, (2 * s + half) * 16 : (2 * s + half) * 16 + 16, cols] = got.astype(BF16).reshape(8, 16, 256)
-
+            got = pltpu.matmul_pop(unit.run(unit.wide[2 * turn + n // 2], [(pick[s], rows)]))
+            packed[:, at, cols] = got.astype(BF16).reshape(8, 16, 256)
+
+    for i in range(16 - lag, 13):
+        hand_on(i)
     for load in weights:
         load.wait()
-    for i in range(16 - lag, 16):
+    for i in range(16):
+        route(0, i, me, other).wait_recv()
+    for half in range(2):
+        pack(0, head_of(me), half)
+        pack(1, head_of(other), half)
+    for i in range(13, 16):
         hand_on(i)
-    for i in range(8):
-        route(0, i, me, other).wait_recv()
-        route(2, i, facing, other).wait_recv()
-    for s in range(4):
-        pack(s, 0)
-    for i in range(8, 16):
-        route(0, i, me, other).wait_recv()
-        route(2, i, facing, other).wait_recv()
-    for s in range(4):
-        pack(s, 1)
+    for half in range(2):
+        for i in range(8 * half, 8 * half + 8):
+            route(2, i, facing, other).wait_recv()
+        pack(0, head_of(facing), half)
+        pack(1, head_of(diagonal), half)
     valid_lane = iota((128, 128), 1) < ACTIONS
     def inner(p):
         accs = []

time: 87 us -> 86.4 us (level)
  no operation moved by 1% of the time
where the time goes in v5:
time: 86.4 us; the launch traced here: 86.3 us
  Pallas kernels  84.4 us (98%)
  local copies, waits for them, and re-layouts  1.26 us (1%)
    pallas_call x1, Pallas kernels, shards(): pl.pallas_call(core_kernel, out_shape=(jax.ShapeDtypeStruct((ACTIONS * 16...  84.4 us

profile of v5, /device:TPU:1, one launch (start us, length us, event | category | flops | bytes accessed | tf_op | source)
XLA Modules:
  0.0 86.3 jit_solution(3840120629108575789)
XLA Ops:
  0.6 84.4 %core.1 = (f32[288,32]{1,0:T(8,128)S(1)}, f32[16,32]{1,0:T(8,128)S(1)}) custom-call(bf16[16,4,256]{2,1,0:T(4,128)(2,1)} %refs_0_.1, bf16[32,4,256]{2,1,0:T(4,128)(2,1)} %refs_1_.1, s32[24,32]{1,0:T(8,128)} %bitcast.14, s32[16,32]{1,0:T(8,128)} %bitcast.15, s32[1,32]{1,0:T(1,128)} %bitcast.16, s32[1,32]{1,0:T(1,128)} %bitcast.17, f32[4,1024]{1,0:T(4,128)} %refs_6_.1, ...), custom_call_target="tpu_custom_call" | custom-call | tf_op jit(solution)/shard_map/core/pallas_call | solution.py:584
  85.0 0.7 copy.17
  85.7 0.6 copy.18

commit v6 on v5

--- a/solution.py
+++ b/solution.py
@@ -64,7 +64,7 @@
     other = {**me, "c": 1 - me["c"]}
     crossed = {k: [] for k in range(3)}
 
-    def region(part, at, free=None, half=None):
+    def region(part, at, free=None, half=None, gates=slice(None)):
         z, x = at["z"], at["x"]
         y = (at["y"] // 2, at["y"] % 2)
         if free == "y":
@@ -72,7 +72,7 @@
         elif free is not None:
             span = slice(None) if half is None else pl.ds(2 * half, 2)
             z, x = (span, x) if free == "z" else (z, span)
-        return full.at[me["c"], z, y[0], y[1], x, :, pl.ds(16 * part, 16), :]
+        return full.at[me["c"], z, y[0], y[1], x, gates, pl.ds(16 * part, 16), :]
 
     def cross(k, ref):
         crossed[k].append(copies.push(ref, other))
@@ -133,7 +133,8 @@
                 for copy in third[k, m, d]:
                     copy.wait_recv()
                 at = shifted(shifted(me, b, offsets[m]), c, -d)
-                relay[k, m, d] = copies.push(region(k, at, free=a, half=(1 - d) // 2), shifted(me, c, d))
+                pair = pl.ds(1 - d, 2)
+                relay[k, m, d] = copies.push(region(k, at, free=a, gates=pair), shifted(me, c, d))
                 cross(k, region(k, at, free=a))
     for m in range(4):
         for k, (a, b, c) in enumerate(ORDERS):

time: 86.4 us -> 86.4 us (level)
  no operation moved by 1% of the time
where the time goes in v6:
time: 86.4 us; the launch traced here: 86.3 us
  Pallas kernels  84.4 us (98%)
  local copies, waits for them, and re-layouts  1.26 us (1%)
    pallas_call x1, Pallas kernels, shards(): pl.pallas_call(core_kernel, out_shape=(jax.ShapeDtypeStruct((ACTIONS * 16...  84.4 us

profile of v6, /device:TPU:1, one launch (start us, length us, event | category | flops | bytes accessed | tf_op | source)
XLA Modules:
  0.0 86.3 jit_solution(3216591989272956828)
XLA Ops:
  0.6 84.4 %core.1 = (f32[288,32]{1,0:T(8,128)S(1)}, f32[16,32]{1,0:T(8,128)S(1)}) custom-call(bf16[16,4,256]{2,1,0:T(4,128)(2,1)} %refs_0_.1, bf16[32,4,256]{2,1,0:T(4,128)(2,1)} %refs_1_.1, s32[24,32]{1,0:T(8,128)} %bitcast.14, s32[16,32]{1,0:T(8,128)} %bitcast.15, s32[1,32]{1,0:T(1,128)} %bitcast.16, s32[1,32]{1,0:T(1,128)} %bitcast.17, f32[4,1024]{1,0:T(4,128)} %refs_6_.1, ...), custom_call_target="tpu_custom_call" | custom-call | tf_op jit(solution)/shard_map/core/pallas_call | solution.py:585
  85.0 0.7 copy.17
  85.7 0.6 copy.18
